TPU v7x, 768 devices: a whole 4x8x12 slice. The times are simulated.
768 devices in a mesh: dp: 12 (over x, z_hi), tensor: 64 (over y, z_lo, core).
Axes of the slice: x: 4, y: 8, z: 12 (z_hi: 3, z_lo: 4; z = z_hi * 4 + z_lo), core: 2. Of those that a mesh axis runs over, the one named last changes fastest.
Arguments:
- queries: bfloat16 [4608, 8192], P('dp', 'tensor'), may hold values from -180 to 180
- keys: bfloat16 [4608, 1024], P('dp'), may hold values from -4.5 to 4.5
- values: bfloat16 [4608, 1024], P('dp'), may hold values from -6 to 6
- grad_out: bfloat16 [4608, 8192], P('dp', 'tensor'), may hold values from -3 to 3
- weight: float32 [8256, 8192], P('dp', 'tensor'), as said below
- first_code: bfloat16 [8256, 8192], P('dp', 'tensor'), may hold values from -1 to 1, as said below
- first_rows: float32 [8256], P('dp'), may hold values from 0.2 to 5
- first_cols: float32 [8192], P('tensor'), may hold values from 0.2 to 5
- second_code: bfloat16 [8256, 8192], P('dp', 'tensor'), may hold values from 0 to 1, as said below
- second_rows: float32 [8256], P('dp'), may hold values from 0.5 to 20
- second_cols: float32 [8192], P('tensor'), may hold values from 0.5 to 20
Outputs:
- grad_queries: bfloat16 [4608, 8192], P('dp', 'tensor')
- new_weight: float32 [8256, 8192], P('dp', 'tensor')
- next_first_code: bfloat16 [8256, 8192], P('dp', 'tensor')
- next_first_rows: float32 [8256], P('dp')
- next_first_cols: float32 [8192], P('tensor')
- next_second_code: bfloat16 [8256, 8192], P('dp', 'tensor')
- next_second_rows: float32 [8256], P('dp')
- next_second_cols: float32 [8192], P('tensor')
Inputs may be any that keep to these rules, and one draw needn't show every extreme that they name: `weight`: rows 8192 onward are zero. `first_code`: rows 8192 onward are zero. `second_code`: rows 8192 onward are zero; all other entries are 0.05 or more.
All inputs are finite; a program needn't handle non-finite values.
Results may differ from a plain program's by a relative error of at most 0.023.
Values may be sent and summed in bfloat16 or wider, within the bound.
No kernel may reach another device: no remote copies, remote signals or barrier semaphores. Data moves between devices by JAX's collectives and lax.ppermute only.
A program may use at most 64 MiB of HBM per device.

v0:
```python
import functools
import jax
import jax.numpy as jnp
from jax import lax
from jax.experimental import pallas as pl
from jax.experimental.pallas import tpu as pltpu
from jax.sharding import Mesh
from jax.sharding import PartitionSpec as P

H = 64
KVH = 8
HD = 128
DP = ("x", "zh")
TENSOR = ("y", "zl", "c")


beta_first = 0.9
beta_second = 0.95
learning = 0.01
decay_rate = 0.1
adam_eps = 1e-08
code_eps = 1e-06
correct_first = 1.0 - 0.9**10
correct_second = 1.0 - 0.95**10
half = jnp.bfloat16
full = jnp.float32
SPILL = 48


def shifted(block, axis, distance):
    size = lax.axis_size(axis)
    return lax.ppermute(block, axis, [(k, (k + distance) % size) for k in range(size)])


def swapped(block, axis, bit):
    size = lax.axis_size(axis)
    return lax.ppermute(block, axis, [(k, k ^ bit) for k in range(size)])


def summed(parts):
    total = parts[0].astype(full)
    for part in parts[1:]:
        total = total + part.astype(full)
    return total


def all_to_all(blocks, axes):
    return lax.all_to_all(blocks, axes, split_axis=0, concat_axis=0, tiled=True)


def attend(queries, key_sel, value_sel):
    shape = (queries.shape[0], key_sel.shape[0])
    scores = jnp.dot(queries, key_sel.T, preferred_element_type=full) * HD ** (-0.5)
    future = lax.broadcasted_iota(jnp.int32, shape, 1) > lax.broadcasted_iota(jnp.int32, shape, 0)
    scores = jnp.where(future, -1e30, scores)
    highest = jnp.max(scores, axis=-1, keepdims=True)
    exponent = jnp.exp(scores - highest)
    probabilities = exponent / jnp.sum(exponent, axis=-1, keepdims=True)
    attended = jnp.dot(probabilities.astype(half), value_sel, preferred_element_type=full)
    return probabilities, attended.astype(half)


def attend_back(probabilities, attended, grad_half, key_sel, value_sel):
    grad_probs = jnp.dot(grad_half, value_sel.T, preferred_element_type=full)
    row_dot = jnp.sum(grad_half.astype(full) * attended.astype(full), axis=-1, keepdims=True)
    grad_scores = (probabilities * (grad_probs - row_dot)).astype(half)
    return (jnp.dot(grad_scores, key_sel, preferred_element_type=full) * HD ** (-0.5)).astype(half)


def group_of(owner, zl, rows):
    return lax.shift_right_arithmetic(owner * rows - zl * (2 * HD) + 6 * HD, 10)


def weight_kernel(zhs, at_ref, weight_ref, own_ref, one_ref, two_ref, padded):
    rows = weight_ref.shape[0]
    owner, zl = at_ref[0] * zhs + at_ref[1], at_ref[2]
    pad = 2 * HD
    padded[...] = jnp.zeros_like(padded)
    padded[pad : pad + rows, :] = weight_ref[...]

    def put(bit, ref):
        place = zl ^ bit
        group = group_of(owner, place, rows)
        for k in range(2):
            start = group * 1024 + place * (2 * HD) + k * HD - owner * rows + pad
            inside = jnp.logical_and(start > pad - HD, start < pad + rows)
            start = pl.multiple_of(jnp.clip(start, 0, pad + rows), 16)
            block = padded[pl.ds(start, HD), :]
            ref[k * HD : (k + 1) * HD, :] = jnp.where(inside, block, 0.0).astype(half)

    put(0, own_ref)
    put(1, one_ref)
    put(2, two_ref.at[0])
    put(3, two_ref.at[1])


def weight_join_kernel(zhs, at_ref, *refs):
    parts, out_ref, scratch = refs[:-2], refs[-2], refs[-1]
    x, zh, zl = at_ref[0], at_ref[1], at_ref[2]
    rows = at_ref[4]
    scratch[...] = jnp.zeros_like(scratch)
    for back, part in enumerate(parts):
        at_zh = zh - back
        at_zh = jnp.where(at_zh < 0, at_zh + zhs, at_zh)
        group = jnp.clip(group_of(x * zhs + at_zh, zl, rows) - 2 * x, 0, 2)
        for h in range(4):
            scratch[group, h] = scratch[group, h] + part[h].astype(full)
    for h in range(4):
        for k in range(2):
            for c in range(2):
                start = (2 * c + k) * HD
                out_ref[h, start : start + HD, :] = scratch[k, h, c * HD : (c + 1) * HD, :].astype(half)
        out_ref[h, 4 * HD :, :] = scratch[2, h, :SPILL, :].astype(half)


def prepare_kernel(grad_ref, out_ref):
    turned = grad_ref[...].T
    for k in range(out_ref.shape[0]):
        out_ref[k] = turned


def out_kernel(at_ref, near_ref, far_ref, att_ref, came_ref, last_ref, out_ref, near_kept, far_kept, scratch, sems):
    core = at_ref[3]
    att = jnp.concatenate([att_ref[...], last_ref[0], came_ref[...], last_ref[1]], axis=1)
    places = out_ref.shape[0]
    scratch[places - 1, 4 * HD :, :] = jnp.zeros((SPILL, out_ref.shape[2]), half)
    copies = [
        pltpu.make_async_copy(near_ref, near_kept, sems.at[places]),
        pltpu.make_async_copy(far_ref, far_kept, sems.at[places + 1]),
    ]
    for copy in copies:
        copy.start()

    def put(part, c, k):
        whole = jnp.dot(part[2 * k : 2 * k + 2].reshape(2 * HD, -1), att, preferred_element_type=full)
        whole = whole.astype(half)
        for y in range(2):
            start = pl.multiple_of(y * 2 * HD + c * HD, HD)
            scratch[k, pl.ds(start, HD), :] = whole[y * HD : (y + 1) * HD]

    for k in range(places - 1, -1, -1):
        put(near_ref, core, k)
        put(far_ref, 1 - core, k)
        if k > 0:
            scratch[k - 1, 4 * HD :, :] = scratch[k, :SPILL, :]
        copy = pltpu.make_async_copy(scratch.at[k], out_ref.at[k], sems.at[k])
        copy.start()
        copies.append(copy)
    for copy in copies:
        copy.wait()


def send_kernel(zhs, at_ref, got_ref, out_ref, padded, sems):
    x, zl, rows = at_ref[0], at_ref[2], at_ref[4]
    sources, count = got_ref.shape[0], got_ref.shape[1]
    padded[count:, :] = jnp.zeros((padded.shape[0] - count, padded.shape[1]), half)

    def piece(r, carry):
        place = pl.ds(pl.multiple_of(r * 16, 16), 16)
        total = got_ref[0, place, :].astype(full)
        for d in range(1, sources):
            total = total + got_ref[d, place, :].astype(full)
        padded[place, :] = total.astype(half)
        return carry

    lax.fori_loop(0, count // 16, piece, 0, unroll=5)
    copies = []
    for z in range(zhs):
        group = jnp.clip(group_of(x * zhs + z, zl, rows) - 2 * x, 0, 2)
        start = pl.multiple_of(group * (2 * HD), 2 * HD)
        for h in range(4):
            block = padded.at[pl.ds(start, 2 * HD), h * HD : (h + 1) * HD]
            copy = pltpu.make_async_copy(block, out_ref.at[z * 4 + (zl ^ h)], sems.at[z * 4 + h])
            copy.start()
            copies.append(copy)
    for copy in copies:
        copy.wait()


def step_kernel(zhs, at_ref, got_ref, *refs):
    far_refs, (new_ref, first_new_ref, second_new_ref, rows_ref, cols_ref, held, padded, sizes, sems) = refs[:3], refs[3:]
    arrivals = [pltpu.make_async_copy(ref, held.at[k], sems.at[k]) for k, ref in enumerate(far_refs)]
    for copy in arrivals:
        copy.start()
    first_ref, second_ref, weight_ref = held.at[0], held.at[1], held.at[2]
    rows = weight_ref.shape[0]
    owner = at_ref[0] * zhs + at_ref[1]
    pad = HD
    padded[...] = jnp.zeros_like(padded)
    for place in range(4):
        total = got_ref[place].astype(full)
        for z in range(1, zhs):
            total = total + got_ref[z * 4 + place].astype(full)
        group = group_of(owner, place, rows)
        for k in range(2):
            start = group * 1024 + place * (2 * HD) + k * HD - owner * rows + pad
            inside = jnp.logical_and(jnp.logical_and(start > 0, start < pad + rows), group < 8)
            start = pl.multiple_of(jnp.where(inside, start, pad + rows), 16)
            padded[pl.ds(start, HD), :] = total[k * HD : (k + 1) * HD]

    per = 16
    for copy in arrivals:
        copy.wait()

    def piece(r, carry):
        place = pl.ds(pl.multiple_of(r * per, per), per)
        grad = padded[pl.ds(pl.multiple_of(r * per + pad, per), per), :]
        first_new = first_ref[place, :] + (1.0 - beta_first) * grad
        second_new = second_ref[place, :] + (1.0 - beta_second) * grad * grad
        size = first_new / correct_first / (jnp.sqrt(second_new / correct_second) + adam_eps)
        weight = weight_ref[place, :]
        new_ref[place, :] = weight - learning * (size + decay_rate * weight)
        first_new_ref[place, :] = first_new
        second_new_ref[place, :] = second_new
        first_abs, second_abs = jnp.abs(first_new), jnp.abs(second_new)
        sizes[0, place, :] = first_abs
        sizes[1, place, :] = second_abs
        return jnp.maximum(carry[0], first_abs), jnp.maximum(carry[1], second_abs)

    start = jnp.zeros((per, HD), full)
    most = lax.fori_loop(0, rows // per, piece, (start, start))
    for m in range(2):
        cols_ref[:, m, :] = jnp.broadcast_to(jnp.max(most[m], axis=0, keepdims=True), (cols_ref.shape[0], HD))
        for block in range(0, rows, HD):
            count = min(HD, rows - block)
            turned = jnp.max(sizes[m, block : block + HD, :].T, axis=0, keepdims=True)
            rows_ref[m : m + 1, block : block + count] = turned[:, :count]


def cot_kernel(at_ref, near_ref, far_ref, *refs):
    weights, out_refs = refs[:4], refs[4:]
    x, core = at_ref[0], at_ref[3]
    dims = (((0,), (0,)), ((), ()))
    groups, _, seq = near_ref.shape
    total = None
    extra_cot, extra_weight = [], []
    for back, weight in enumerate(weights):
        at_x = x - back
        at_x = jnp.where(at_x < 0, at_x + len(weights), at_x)
        wide = jnp.concatenate([weight[h] for h in range(4)], axis=1)
        for c in range(2):
            own, other = near_ref[pl.ds(2 * at_x, 2)], far_ref[pl.ds(2 * at_x, 2)]
            cot = jnp.where(core == c, own, other).reshape(2 * HD, seq)
            start = 2 * c * HD
            term = lax.dot_general(cot, wide[start : start + 2 * HD], dims, preferred_element_type=full)
            total = term if total is None else total + term
        y = jnp.minimum(2 * at_x + 2, groups - 1)
        extra_cot.append(jnp.where(core == 0, near_ref[y, :SPILL, :], far_ref[y, :SPILL, :]))
        extra_weight.append(wide[4 * HD :])
    extra_cot, extra_weight = jnp.concatenate(extra_cot, axis=0), jnp.concatenate(extra_weight, axis=0)
    total = total + lax.dot_general(extra_cot, extra_weight, dims, preferred_element_type=full)
    total = total.astype(half)
    out_refs[0][...] = total[:, :HD]
    out_refs[1][...] = total[:, HD : 2 * HD]
    out_refs[2][0] = total[:, 2 * HD : 3 * HD]
    out_refs[2][1] = total[:, 3 * HD :]


def step(
    queries,
    keys,
    values,
    grad_out,
    weight,
    first_code,
    first_rows,
    first_cols,
    second_code,
    second_rows,
    second_cols,
):
    dp_count = lax.axis_size(DP)
    ys, zls = lax.axis_size("y"), lax.axis_size("zl")
    xs, zhs = lax.axis_size("x"), lax.axis_size("zh")
    seq = queries.shape[0]
    rows = weight.shape[0]
    kv_start = lax.axis_index(TENSOR) // (H // KVH) * HD
    at = jnp.stack([lax.axis_index(axis) for axis in ("x", "zh", "zl", "c")] + [rows]).astype(jnp.int32)
    smem, vmem = pl.BlockSpec(memory_space=pltpu.SMEM), pl.BlockSpec(memory_space=pltpu.VMEM)
    shape = jax.ShapeDtypeStruct

    def kernel(body, arguments, outs, flops, room, scratch=(), space=vmem, spaces=None):
        return pl.pallas_call(
            body,
            out_shape=outs,
            in_specs=[smem] + (spaces or [vmem] * len(arguments)),
            out_specs=jax.tree.map(lambda _: space, outs),
            scratch_shapes=scratch,
            compiler_params=pltpu.CompilerParams(vmem_limit_bytes=room * 1024 * 1024),
            cost_estimate=pl.CostEstimate(flops=flops, bytes_accessed=3000000, transcendentals=0),
        )(at, *arguments)

    cot = pl.pallas_call(
        prepare_kernel,
        out_shape=shape((ys, HD, seq), half),
        compiler_params=pltpu.CompilerParams(vmem_limit_bytes=4 * 1024 * 1024),
    )(grad_out)
    near = all_to_all(cot, "y")
    far = shifted(near, "c", 1)

    own, one, two = kernel(
        functools.partial(weight_kernel, zhs),
        (weight,),
        (shape((2 * HD, HD), half), shape((2 * HD, HD), half), shape((2, 2 * HD, HD), half)),
        10000000,
        4,
        [pltpu.VMEM((rows + 4 * HD, HD), full)],
    )
    came = swapped(two, "zl", 2)
    last = swapped(jnp.stack([one, came[1]]), "zl", 1)
    part = jnp.stack([own, last[0], came[0], last[1]])

    key_sel = lax.dynamic_slice_in_dim(keys, kv_start, HD, 1)
    value_sel = lax.dynamic_slice_in_dim(values, kv_start, HD, 1)
    probabilities, attended = attend(queries, key_sel, value_sel)
    attended, probabilities = lax.optimization_barrier((attended, probabilities))
    came = swapped(attended, "zl", 2)
    last = swapped(jnp.stack([attended, came]), "zl", 1)

    hbm = pl.BlockSpec(memory_space=pltpu.HBM)
    in_hbm = functools.partial(pltpu.with_memory_space_constraint, memory_space=pltpu.HBM)
    cut = 4 * HD + SPILL
    kept = pltpu.HBM((ys, HD, seq), half)
    partial, near, far = kernel(
        out_kernel,
        (near, far, attended, came, last),
        (pltpu.HBM((xs, cut, zls * HD), half), kept, kept),
        800000000,
        16,
        [pltpu.VMEM((xs, cut, zls * HD), half), pltpu.SemaphoreType.DMA((xs + 2,))],
        hbm,
    )
    partial = all_to_all(partial, "x")
    partial = kernel(
        functools.partial(send_kernel, zhs),
        (partial,),
        pltpu.HBM((zhs * zls, 2 * HD, HD), half),
        10000000,
        10,
        [pltpu.VMEM((6 * HD, zls * HD), half), pltpu.SemaphoreType.DMA((zhs * zls,))],
        hbm,
    )
    partial = all_to_all(partial, ("zh", "zl"))
    first = beta_first * (first_code.astype(full) * jnp.minimum(first_rows[:, None], first_cols[None, :]))
    second = beta_second * (second_code.astype(full) * jnp.minimum(second_rows[:, None], second_cols[None, :]))
    moment = pltpu.HBM((rows, HD), full)
    new_weight, first_new, second_new, rows_max, cols_max = kernel(
        functools.partial(step_kernel, zhs),
        (partial, in_hbm(first), in_hbm(second), in_hbm(weight)),
        (moment, moment, moment, shape((2, rows), full), pltpu.HBM((dp_count, 2, HD), full)),
        10000000,
        8,
        [
            pltpu.VMEM((3, rows, HD), full),
            pltpu.VMEM((rows + 3 * HD, HD), full),
            pltpu.VMEM((2, -(-rows // HD) * HD, HD), full),
            pltpu.SemaphoreType.DMA((3,)),
        ],
        vmem,
        [vmem] + [hbm] * 3,
    )
    cols_max = jnp.max(all_to_all(cols_max, DP), axis=0)
    rows_max = jnp.max(lax.all_gather(rows_max, "c"), axis=0)
    rows_max = jnp.broadcast_to(rows_max[None], (ys * zls, *rows_max.shape))
    rows_max = jnp.max(all_to_all(rows_max, ("y", "zl")), axis=0)
    next_first_code = (
        first_new / (jnp.minimum(rows_max[0][:, None], cols_max[0][None, :]) + code_eps)
    ).astype(half)
    next_second_code = (
        second_new / (jnp.minimum(rows_max[1][:, None], cols_max[1][None, :]) + code_eps)
    ).astype(half)

    parts = [part] + [shifted(part, "zh", d) for d in range(1, zhs)]
    part = kernel(
        functools.partial(weight_join_kernel, zhs),
        parts,
        shape((zls, 4 * HD + SPILL, HD), half),
        10000000,
        6,
        [pltpu.VMEM((3, zls, 2 * HD, HD), full)],
    )
    before = shifted(part, "x", 1)
    after = shifted(part, "x", 3)
    parts = [part, before, shifted(before, "x", 1), after]
    own, one, two = kernel(
        cot_kernel,
        (near, far, *parts),
        (shape((seq, HD), half), shape((seq, HD), half), shape((2, seq, HD), half)),
        800000000,
        16,
    )
    came = swapped(two, "zl", 2)
    mid = summed([one, came[1]]).astype(half)
    last = swapped(mid, "zl", 1)
    grad_half = summed([own, came[0], last]).astype(half)
    grad_queries = attend_back(probabilities, attended, grad_half, key_sel, value_sel)
    return (
        grad_queries,
        new_weight,
        next_first_code,
        rows_max[0],
        cols_max[0],
        next_second_code,
        rows_max[1],
        cols_max[1],
    )


def solution(mesh):
    finer = Mesh(mesh.devices.reshape(4, 3, 8, 4, 2), (*DP, *TENSOR))
    placed = (
        P(DP, TENSOR),
        P(DP, None),
        P(DP, None),
        P(DP, TENSOR),
        P(DP, TENSOR),
        P(DP, TENSOR),
        P(DP),
        P(TENSOR),
        P(DP, TENSOR),
        P(DP),
        P(TENSOR),
    )
    return jax.shard_map(
        step,
        mesh=finer,
        in_specs=placed,
        out_specs=(
            P(DP, TENSOR),
            P(DP, TENSOR),
            P(DP, TENSOR),
            P(DP),
            P(TENSOR),
            P(DP, TENSOR),
            P(DP),
            P(TENSOR),
        ),
        check_vma=False,
    )
```

profile of v0, /device:TPU:2, one launch (start us, length us, event | category | flops | bytes accessed | tf_op | source)
XLA Modules:
  0.0 215.0 jit_solution(13764346253250496163)
XLA Ops:
  2.6 7.1 %all-to-all-start = ((bf16[8,128,384]{2,1,0:T(8,128)(2,1)}), bf16[8,128,384]{2,1,0:T(8,128)(2,1)S(1)}, u32[]{:S(2)}, u32[]{:S(2)}) async-start(bf16[8,128,384]{2,1,0:T(8,128)(2,1)} %shard_map.170), calls=%async_computation | async-start | bytes 1572864 | tf_op jit(solution)/shard_map/all_to_all | solution.py:48
  12.0 20.8 %all-to-all-done.near_ref = bf16[8,128,384]{2,1,0:T(8,128)(2,1)S(1)} async-done(((bf16[8,128,384]{2,1,0:T(8,128)(2,1)}), bf16[8,128,384]{2,1,0:T(8,128)(2,1)S(1)}, u32[]{:S(2)}, u32[]{:S(2)}) %all-to-all-start) | async-done | bytes 786464 | tf_op jit(solution)/shard_map/all_to_all | solution.py:48
  37.2 6.1 %collective-permute-start.1 = (bf16[384,128]{1,0:T(8,128)(2,1)S(1)}, bf16[384,128]{1,0:T(8,128)(2,1)S(1)}, u32[]{:S(2)}, u32[]{:S(2)}) collective-permute-start(bf16[384,128]{1,0:T(8,128)(2,1)S(1)} %convolution_convert_fusion.att_ref), channel_id=1, source_target_pairs={{0,4},{2,6},{4,0},{6,2},{1,5},{3,7},{5,1},{7,3},{8,12},{10,14},{12... | collective-permute-start | bytes 294920 | tf_op jit(solution)/shard_map/ppermute | solution.py:37
  43.3 5.5 %collective-permute-done.1.came_ref = bf16[384,128]{1,0:T(8,128)(2,1)S(1)} collective-permute-done((bf16[384,128]{1,0:T(8,128)(2,1)S(1)}, bf16[384,128]{1,0:T(8,128)(2,1)S(1)}, u32[]{:S(2)}, u32[]{:S(2)}) %collective-permute-start.1) | collective-permute-done | bytes 98336 | tf_op jit(solution)/shard_map/ppermute | solution.py:37
  51.7 5.0 %collective-permute-done.2.last_ref = bf16[2,384,128]{2,1,0:T(8,128)(2,1)S(1)} collective-permute-done((bf16[2,384,128]{2,1,0:T(8,128)(2,1)S(1)}, bf16[2,384,128]{2,1,0:T(8,128)(2,1)S(1)}, u32[]{:S(2)}, u32[]{:S(2)}) %collective-permute-start.2) | collective-permute-done | bytes 196640 | tf_op jit(solution)/shard_map/ppermute | solution.py:37
  59.4 5.0 %all-to-all-start.1 = ((bf16[4,560,512]{2,1,0:T(8,128)(2,1)}), bf16[4,560,512]{2,1,0:T(8,128)(2,1)S(1)}, u32[]{:S(2)}, u32[]{:S(2)}) async-start(bf16[4,560,512]{2,1,0:T(8,128)(2,1)} %get-tuple-element.34), calls=%async_computation.1 | async-start | bytes 4587520 | tf_op jit(solution)/shard_map/all_to_all | solution.py:48
  65.0 5.3 %collective-permute-start.3 = (bf16[2,256,128]{2,1,0:T(8,128)(2,1)S(1)}, bf16[2,256,128]{2,1,0:T(8,128)(2,1)S(1)}, u32[]{:S(2)}, u32[]{:S(2)}) collective-permute-start(bf16[2,256,128]{2,1,0:T(8,128)(2,1)S(1)} %get-tuple-element.30), channel_id=1, source_target_pairs={{0,4},{2,6},{4,0},{6,2},{1,5},{3,7},{5,1},{7,3},{8,12},{10,14},{12... | collective-permute-start | bytes 393224 | tf_op jit(solution)/shard_map/ppermute | solution.py:37
  70.3 5.4 %collective-permute-done.3 = bf16[2,256,128]{2,1,0:T(8,128)(2,1)S(1)} collective-permute-done((bf16[2,256,128]{2,1,0:T(8,128)(2,1)S(1)}, bf16[2,256,128]{2,1,0:T(8,128)(2,1)S(1)}, u32[]{:S(2)}, u32[]{:S(2)}) %collective-permute-start.3) | collective-permute-done | bytes 131104 | tf_op jit(solution)/shard_map/ppermute | solution.py:37
  78.3 4.2 %collective-permute-done.4 = bf16[2,256,128]{2,1,0:T(8,128)(2,1)S(1)} collective-permute-done((bf16[2,256,128]{2,1,0:T(8,128)(2,1)S(1)}, bf16[2,256,128]{2,1,0:T(8,128)(2,1)S(1)}, u32[]{:S(2)}, u32[]{:S(2)}) %collective-permute-start.4) | collective-permute-done | bytes 131104 | tf_op jit(solution)/shard_map/ppermute | solution.py:37
  82.6 10.9 %collective-permute-start.5 = (bf16[4,256,128]{2,1,0:T(8,128)(2,1)S(1)}, bf16[4,256,128]{2,1,0:T(8,128)(2,1)}, u32[]{:S(2)}, u32[]{:S(2)}) collective-permute-start(bf16[4,256,128]{2,1,0:T(8,128)(2,1)S(1)} %pad_maximum_fusion.refs_0_), channel_id=1, source_target_pairs={{0,64},{64,128},{128,0},{1,65},{65,129},{129,1},{2,66},{66,130},{1... | collective-permute-start | bytes 786440 | tf_op jit(solution)/shard_map/ppermute | solution.py:32
  93.6 3.8 %collective-permute-start.6 = (bf16[4,256,128]{2,1,0:T(8,128)(2,1)S(1)}, bf16[4,256,128]{2,1,0:T(8,128)(2,1)}, u32[]{:S(2)}, u32[]{:S(2)}) collective-permute-start(bf16[4,256,128]{2,1,0:T(8,128)(2,1)S(1)} %pad_maximum_fusion.refs_0_), channel_id=1, source_target_pairs={{0,128},{64,0},{128,64},{1,129},{65,1},{129,65},{2,130},{66,2},{13... | collective-permute-start | bytes 786440 | tf_op jit(solution)/shard_map/ppermute | solution.py:32
  99.2 8.2 %all-to-all-start.2 = ((bf16[12,256,128]{2,1,0:T(8,128)(2,1)}), bf16[12,256,128]{2,1,0:T(8,128)(2,1)S(1)}, u32[]{:S(2)}, u32[]{:S(2)}) async-start(bf16[12,256,128]{2,1,0:T(8,128)(2,1)} %shard_map.175), calls=%async_computation.2 | async-start | bytes 1572864 | tf_op jit(solution)/shard_map/all_to_all | solution.py:48
  107.5 13.9 %collective-permute-done.6.refs_2_ = bf16[4,256,128]{2,1,0:T(8,128)(2,1)} collective-permute-done((bf16[4,256,128]{2,1,0:T(8,128)(2,1)S(1)}, bf16[4,256,128]{2,1,0:T(8,128)(2,1)}, u32[]{:S(2)}, u32[]{:S(2)}) %collective-permute-start.6) | collective-permute-done | bytes 262176 | tf_op jit(solution)/shard_map/ppermute | solution.py:32
  122.7 5.9 %collective-permute-start.7 = (bf16[4,560,128]{2,1,0:T(8,128)(2,1)S(1)}, bf16[4,560,128]{2,1,0:T(8,128)(2,1)S(1)}, u32[]{:S(2)}, u32[]{:S(2)}) collective-permute-start(bf16[4,560,128]{2,1,0:T(8,128)(2,1)S(1)} %shard_map.173.refs_0_), channel_id=1, source_target_pairs={{0,192},{192,384},{384,576},{576,0},{1,193},{193,385},{385,577},{5... | collective-permute-start | bytes 1720328 | tf_op jit(solution)/shard_map/ppermute | solution.py:32
  130.6 9.2 %collective-permute-done.7.refs_1_ = bf16[4,560,128]{2,1,0:T(8,128)(2,1)S(1)} collective-permute-done((bf16[4,560,128]{2,1,0:T(8,128)(2,1)S(1)}, bf16[4,560,128]{2,1,0:T(8,128)(2,1)S(1)}, u32[]{:S(2)}, u32[]{:S(2)}) %collective-permute-start.7) | collective-permute-done | bytes 573472 | tf_op jit(solution)/shard_map/ppermute | solution.py:32
  139.8 4.4 %collective-permute-start.8 = (bf16[4,560,128]{2,1,0:T(8,128)(2,1)S(1)}, bf16[4,560,128]{2,1,0:T(8,128)(2,1)S(1)}, u32[]{:S(2)}, u32[]{:S(2)}) collective-permute-start(bf16[4,560,128]{2,1,0:T(8,128)(2,1)S(1)} %collective-permute-done.7.refs_1_), channel_id=1, source_target_pairs={{0,192},{192,384},{384,576},{576,0},{1,193},{193,385},{385,577},{5... | collective-permute-start | bytes 1720328 | tf_op jit(solution)/shard_map/ppermute | solution.py:32
  144.2 11.4 %collective-permute-done.8.refs_2_ = bf16[4,560,128]{2,1,0:T(8,128)(2,1)S(1)} collective-permute-done((bf16[4,560,128]{2,1,0:T(8,128)(2,1)S(1)}, bf16[4,560,128]{2,1,0:T(8,128)(2,1)S(1)}, u32[]{:S(2)}, u32[]{:S(2)}) %collective-permute-start.8) | collective-permute-done | bytes 573472 | tf_op jit(solution)/shard_map/ppermute | solution.py:32
  158.4 7.3 %collective-permute-start.10 = (bf16[2,384,128]{2,1,0:T(8,128)(2,1)S(1)}, bf16[2,384,128]{2,1,0:T(8,128)(2,1)S(1)}, u32[]{:S(2)}, u32[]{:S(2)}) collective-permute-start(bf16[2,384,128]{2,1,0:T(8,128)(2,1)S(1)} %get-tuple-element.32), channel_id=1, source_target_pairs={{0,4},{2,6},{4,0},{6,2},{1,5},{3,7},{5,1},{7,3},{8,12},{10,14},{12... | collective-permute-start | bytes 589832 | tf_op jit(solution)/shard_map/ppermute | solution.py:37
  166.6 3.0 %collective-permute-done.10 = bf16[2,384,128]{2,1,0:T(8,128)(2,1)S(1)} collective-permute-done((bf16[2,384,128]{2,1,0:T(8,128)(2,1)S(1)}, bf16[2,384,128]{2,1,0:T(8,128)(2,1)S(1)}, u32[]{:S(2)}, u32[]{:S(2)}) %collective-permute-start.10) | collective-permute-done | bytes 196640 | tf_op jit(solution)/shard_map/ppermute | solution.py:37
  172.6 3.8 %shard_map.176 = (f32[688,128]{1,0:T(8,128)}, f32[688,128]{1,0:T(8,128)}, f32[688,128]{1,0:T(8,128)}, f32[2,688]{1,0:T(2,128)S(1)}, f32[12,2,128]{2,1,0:T(2,128)}) custom-call(s32[5]{0:T(128)S(1)} %stack.40.at_ref, bf16[12,256,128]{2,1,0:T(8,128)(2,1)S(1)} %all-to-all-done.2.got_ref, f32[688,128]{1,0:T(8,128)} %multiply_multiply_fusion.1.refs_0_, ...), custom_call_target="tpu_custom_call" | custom-call | flops 10000000 | bytes 3000000 | tf_op jit(solution)/shard_map/pallas_call | solution.py:283
  176.4 11.9 %all-to-all-start.4 = ((f32[12,2,128]{2,1,0:T(2,128)}), f32[12,2,128]{2,1,0:T(2,128)S(1)}, u32[]{:S(2)}, u32[]{:S(2)}) async-start(f32[12,2,128]{2,1,0:T(2,128)} %get-tuple-element.38), calls=%async_computation.4 | async-start | bytes 24576 | tf_op jit(solution)/shard_map/all_to_all | solution.py:48
  190.2 6.9 %all-to-all-done.4 = f32[12,2,128]{2,1,0:T(2,128)S(1)} async-done(((f32[12,2,128]{2,1,0:T(2,128)}), f32[12,2,128]{2,1,0:T(2,128)S(1)}, u32[]{:S(2)}, u32[]{:S(2)}) %all-to-all-start.4) | async-done | bytes 12320 | tf_op jit(solution)/shard_map/all_to_all | solution.py:48
  197.8 4.6 %all-to-all-start.3 = ((f32[32,2,688]{2,1,0:T(2,128)}), f32[32,2,688]{2,1,0:T(2,128)S(1)}, u32[]{:S(2)}, u32[]{:S(2)}) async-start(f32[32,2,688]{2,1,0:T(2,128)} %broadcast_in_dim.7), calls=%async_computation.3 | async-start | bytes 393216 | tf_op jit(solution)/shard_map/all_to_all | solution.py:48
  204.6 9.2 %all-to-all-done.3 = f32[32,2,688]{2,1,0:T(2,128)S(1)} async-done(((f32[32,2,688]{2,1,0:T(2,128)}), f32[32,2,688]{2,1,0:T(2,128)S(1)}, u32[]{:S(2)}, u32[]{:S(2)}) %all-to-all-start.3) | async-done | bytes 176160 | tf_op jit(solution)/shard_map/all_to_all | solution.py:48
  (80 shorter events, 35.0 us)
Async XLA Ops:
  2.6 30.2 %all-to-all-start = ((bf16[8,128,384]{2,1,0:T(8,128)(2,1)}), bf16[8,128,384]{2,1,0:T(8,128)(2,1)S(1)}, u32[]{:S(2)}, u32[]{:S(2)}) async-start(bf16[8,128,384]{2,1,0:T(8,128)(2,1)} %shard_map.170), calls=%async_computation | async-start | bytes 1572864 | tf_op jit(solution)/shard_map/all_to_all | solution.py:48
  32.8 23.8 %collective-permute-start = (bf16[8,128,384]{2,1,0:T(8,128)(2,1)S(1)}, bf16[8,128,384]{2,1,0:T(8,128)(2,1)S(1)}, u32[]{:S(2)}, u32[]{:S(2)}) collective-permute-start(bf16[8,128,384]{2,1,0:T(8,128)(2,1)S(1)} %all-to-all-done.near_ref), channel_id=1, source_target_pairs={{0,1},{1,0},{2,3},{3,2},{4,5},{5,4},{6,7},{7,6},{8,9},{9,8},{10,11... | collective-permute-start | bytes 2359304 | tf_op jit(solution)/shard_map/ppermute | solution.py:32
  37.2 11.6 %collective-permute-start.1 = (bf16[384,128]{1,0:T(8,128)(2,1)S(1)}, bf16[384,128]{1,0:T(8,128)(2,1)S(1)}, u32[]{:S(2)}, u32[]{:S(2)}) collective-permute-start(bf16[384,128]{1,0:T(8,128)(2,1)S(1)} %convolution_convert_fusion.att_ref), channel_id=1, source_target_pairs={{0,4},{2,6},{4,0},{6,2},{1,5},{3,7},{5,1},{7,3},{8,12},{10,14},{12... | collective-permute-start | bytes 294920 | tf_op jit(solution)/shard_map/ppermute | solution.py:37
  48.9 7.8 %collective-permute-start.2 = (bf16[2,384,128]{2,1,0:T(8,128)(2,1)S(1)}, bf16[2,384,128]{2,1,0:T(8,128)(2,1)S(1)}, u32[]{:S(2)}, u32[]{:S(2)}) collective-permute-start(bf16[2,384,128]{2,1,0:T(8,128)(2,1)S(1)} %pad_maximum_fusion.1), channel_id=1, source_target_pairs={{0,2},{2,0},{4,6},{6,4},{1,3},{3,1},{5,7},{7,5},{8,10},{10,8},{12,... | collective-permute-start | bytes 589832 | tf_op jit(solution)/shard_map/ppermute | solution.py:37
  59.4 38.0 %all-to-all-start.1 = ((bf16[4,560,512]{2,1,0:T(8,128)(2,1)}), bf16[4,560,512]{2,1,0:T(8,128)(2,1)S(1)}, u32[]{:S(2)}, u32[]{:S(2)}) async-start(bf16[4,560,512]{2,1,0:T(8,128)(2,1)} %get-tuple-element.34), calls=%async_computation.1 | async-start | bytes 4587520 | tf_op jit(solution)/shard_map/all_to_all | solution.py:48
  65.0 10.7 %collective-permute-start.3 = (bf16[2,256,128]{2,1,0:T(8,128)(2,1)S(1)}, bf16[2,256,128]{2,1,0:T(8,128)(2,1)S(1)}, u32[]{:S(2)}, u32[]{:S(2)}) collective-permute-start(bf16[2,256,128]{2,1,0:T(8,128)(2,1)S(1)} %get-tuple-element.30), channel_id=1, source_target_pairs={{0,4},{2,6},{4,0},{6,2},{1,5},{3,7},{5,1},{7,3},{8,12},{10,14},{12... | collective-permute-start | bytes 393224 | tf_op jit(solution)/shard_map/ppermute | solution.py:37
  75.7 6.9 %collective-permute-start.4 = (bf16[2,256,128]{2,1,0:T(8,128)(2,1)S(1)}, bf16[2,256,128]{2,1,0:T(8,128)(2,1)S(1)}, u32[]{:S(2)}, u32[]{:S(2)}) collective-permute-start(bf16[2,256,128]{2,1,0:T(8,128)(2,1)S(1)} %pad_maximum_fusion.2), channel_id=1, source_target_pairs={{0,2},{2,0},{4,6},{6,4},{1,3},{3,1},{5,7},{7,5},{8,10},{10,8},{12,... | collective-permute-start | bytes 393224 | tf_op jit(solution)/shard_map/ppermute | solution.py:37
  82.6 24.9 %collective-permute-start.5 = (bf16[4,256,128]{2,1,0:T(8,128)(2,1)S(1)}, bf16[4,256,128]{2,1,0:T(8,128)(2,1)}, u32[]{:S(2)}, u32[]{:S(2)}) collective-permute-start(bf16[4,256,128]{2,1,0:T(8,128)(2,1)S(1)} %pad_maximum_fusion.refs_0_), channel_id=1, source_target_pairs={{0,64},{64,128},{128,0},{1,65},{65,129},{129,1},{2,66},{66,130},{1... | collective-permute-start | bytes 786440 | tf_op jit(solution)/shard_map/ppermute | solution.py:32
  93.6 27.8 %collective-permute-start.6 = (bf16[4,256,128]{2,1,0:T(8,128)(2,1)S(1)}, bf16[4,256,128]{2,1,0:T(8,128)(2,1)}, u32[]{:S(2)}, u32[]{:S(2)}) collective-permute-start(bf16[4,256,128]{2,1,0:T(8,128)(2,1)S(1)} %pad_maximum_fusion.refs_0_), channel_id=1, source_target_pairs={{0,128},{64,0},{128,64},{1,129},{65,1},{129,65},{2,130},{66,2},{13... | collective-permute-start | bytes 786440 | tf_op jit(solution)/shard_map/ppermute | solution.py:32
  99.2 56.4 %copy-start.2 = (bf16[8,128,384]{2,1,0:T(8,128)(2,1)S(1)}, bf16[8,128,384]{2,1,0:T(8,128)(2,1)}, u32[]{:S(2)}) copy-start(bf16[8,128,384]{2,1,0:T(8,128)(2,1)} %get-tuple-element.26.near_ref) | copy-start | bytes 2359300
  99.2 73.3 %all-to-all-start.2 = ((bf16[12,256,128]{2,1,0:T(8,128)(2,1)}), bf16[12,256,128]{2,1,0:T(8,128)(2,1)S(1)}, u32[]{:S(2)}, u32[]{:S(2)}) async-start(bf16[12,256,128]{2,1,0:T(8,128)(2,1)} %shard_map.175), calls=%async_computation.2 | async-start | bytes 1572864 | tf_op jit(solution)/shard_map/all_to_all | solution.py:48
  107.4 58.3 %copy-start.9 = (bf16[688,128]{1,0:T(8,128)(2,1)S(1)}, bf16[688,128]{1,0:T(8,128)(2,1)}, u32[]{:S(2)}) copy-start(bf16[688,128]{1,0:T(8,128)(2,1)} %param.19) | copy-start | bytes 528388
  107.5 58.3 %copy-start.13 = (f32[688]{0:T(1024)S(1)}, f32[688]{0:T(1024)}, u32[]{:S(2)}) copy-start(f32[688]{0:T(1024)} %param.20) | copy-start | bytes 8260
  107.5 58.3 %copy-start.17 = (f32[128]{0:T(128)S(1)}, f32[128]{0:T(128)}, u32[]{:S(2)}) copy-start(f32[128]{0:T(128)} %param.21) | copy-start | bytes 1540
  122.7 17.1 %collective-permute-start.7 = (bf16[4,560,128]{2,1,0:T(8,128)(2,1)S(1)}, bf16[4,560,128]{2,1,0:T(8,128)(2,1)S(1)}, u32[]{:S(2)}, u32[]{:S(2)}) collective-permute-start(bf16[4,560,128]{2,1,0:T(8,128)(2,1)S(1)} %shard_map.173.refs_0_), channel_id=1, source_target_pairs={{0,192},{192,384},{384,576},{576,0},{1,193},{193,385},{385,577},{5... | collective-permute-start | bytes 1720328 | tf_op jit(solution)/shard_map/ppermute | solution.py:32
  128.7 15.6 %collective-permute-start.9 = (bf16[4,560,128]{2,1,0:T(8,128)(2,1)S(1)}, bf16[4,560,128]{2,1,0:T(8,128)(2,1)S(1)}, u32[]{:S(2)}, u32[]{:S(2)}) collective-permute-start(bf16[4,560,128]{2,1,0:T(8,128)(2,1)S(1)} %shard_map.173.refs_0_), channel_id=1, source_target_pairs={{0,576},{192,0},{384,192},{576,384},{1,577},{193,1},{385,193},{577... | collective-permute-start | bytes 1720328 | tf_op jit(solution)/shard_map/ppermute | solution.py:32
  139.8 15.8 %collective-permute-start.8 = (bf16[4,560,128]{2,1,0:T(8,128)(2,1)S(1)}, bf16[4,560,128]{2,1,0:T(8,128)(2,1)S(1)}, u32[]{:S(2)}, u32[]{:S(2)}) collective-permute-start(bf16[4,560,128]{2,1,0:T(8,128)(2,1)S(1)} %collective-permute-done.7.refs_1_), channel_id=1, source_target_pairs={{0,192},{192,384},{384,576},{576,0},{1,193},{193,385},{385,577},{5... | collective-permute-start | bytes 1720328 | tf_op jit(solution)/shard_map/ppermute | solution.py:32
  158.4 44.1 %copy-start.6 = (f32[384,384]{0,1:T(8,128)S(1)}, f32[384,384]{0,1:T(8,128)}, u32[]{:S(2)}) copy-start(f32[384,384]{0,1:T(8,128)} %copy-done.5) | copy-start | bytes 1769476
  158.4 11.2 %collective-permute-start.10 = (bf16[2,384,128]{2,1,0:T(8,128)(2,1)S(1)}, bf16[2,384,128]{2,1,0:T(8,128)(2,1)S(1)}, u32[]{:S(2)}, u32[]{:S(2)}) collective-permute-start(bf16[2,384,128]{2,1,0:T(8,128)(2,1)S(1)} %get-tuple-element.32), channel_id=1, source_target_pairs={{0,4},{2,6},{4,0},{6,2},{1,5},{3,7},{5,1},{7,3},{8,12},{10,14},{12... | collective-permute-start | bytes 589832 | tf_op jit(solution)/shard_map/ppermute | solution.py:37
  169.7 32.6 %collective-permute-start.11 = (bf16[384,128]{1,0:T(8,128)(2,1)S(1)}, bf16[384,128]{1,0:T(8,128)(2,1)S(1)}, u32[]{:S(2)}, u32[]{:S(2)}) collective-permute-start(bf16[384,128]{1,0:T(8,128)(2,1)S(1)} %fusion.11), channel_id=1, source_target_pairs={{0,2},{2,0},{4,6},{6,4},{1,3},{3,1},{5,7},{7,5},{8,10},{10,8},{12,... | collective-permute-start | bytes 294920 | tf_op jit(solution)/shard_map/ppermute | solution.py:37
  176.4 37.6 %copy-start.7 = (f32[688,128]{1,0:T(8,128)S(1)}, f32[688,128]{1,0:T(8,128)}, u32[]{:S(2)}) copy-start(f32[688,128]{1,0:T(8,128)} %get-tuple-element.36) | copy-start | bytes 1056772
  176.4 37.6 %copy-start.8 = (f32[688,128]{1,0:T(8,128)S(1)}, f32[688,128]{1,0:T(8,128)}, u32[]{:S(2)}) copy-start(f32[688,128]{1,0:T(8,128)} %get-tuple-element.39) | copy-start | bytes 1056772
  176.4 20.6 %all-to-all-start.4 = ((f32[12,2,128]{2,1,0:T(2,128)}), f32[12,2,128]{2,1,0:T(2,128)S(1)}, u32[]{:S(2)}, u32[]{:S(2)}) async-start(f32[12,2,128]{2,1,0:T(2,128)} %get-tuple-element.38), calls=%async_computation.4 | async-start | bytes 24576 | tf_op jit(solution)/shard_map/all_to_all | solution.py:48
  197.8 16.1 %all-to-all-start.3 = ((f32[32,2,688]{2,1,0:T(2,128)}), f32[32,2,688]{2,1,0:T(2,128)S(1)}, u32[]{:S(2)}, u32[]{:S(2)}) async-start(f32[32,2,688]{2,1,0:T(2,128)} %broadcast_in_dim.7), calls=%async_computation.3 | async-start | bytes 393216 | tf_op jit(solution)/shard_map/all_to_all | solution.py:48
  (13 other events, 104.8 us)
where the time goes:
time: 216 us; the launch traced here: 215 us
  waiting for transfers between devices  94.6 us (44%)
  starting transfers between devices  91.4 us (42%)
  Pallas kernels  13 us (6%)
  other arithmetic  5.49 us (3%)
  matrix products  4.41 us (2%)
  local copies, waits for them, and re-layouts  3.05 us (1%)
    all_to_all x5, waiting for transfers between devices, all_to_all(): return lax.all_to_all(blocks, axes, split_axis=0, concat_axis=0, tiled=True)  36.9 us
    all_to_all x5, starting transfers between devices, all_to_all(): return lax.all_to_all(blocks, axes, split_axis=0, concat_axis=0, tiled=True)  36.8 us
    ppermute x6, waiting for transfers between devices, shifted(): lax.ppermute(block, axis, [(k, (k + distance) % size) for k in range(size)])  34.5 us
    ppermute x6, starting transfers between devices, shifted(): lax.ppermute(block, axis, [(k, (k + distance) % size) for k in range(size)])  28.8 us
    ppermute x6, starting transfers between devices, swapped(): return lax.ppermute(block, axis, [(k, k ^ bit) for k in range(size)])  25.8 us
    ppermute x6, waiting for transfers between devices, swapped(): return lax.ppermute(block, axis, [(k, k ^ bit) for k in range(size)])  23.2 us
    pallas_call x6, Pallas kernels, kernel(): pl.pallas_call(body, out_shape=outs, in_specs=[smem] + (spaces or [vmem]...  12 us
  transfers between devices with their start and end apart: 17, of which 11 were waited for; matrix products, arithmetic and copies ran while one was open for 4% of the time, Pallas kernels for 4%

commit v1 on v0

--- a/solution.py
+++ b/solution.py
@@ -218,7 +218,7 @@
         return jnp.maximum(carry[0], first_abs), jnp.maximum(carry[1], second_abs)
 
     start = jnp.zeros((per, HD), full)
-    most = lax.fori_loop(0, rows // per, piece, (start, start))
+    most = lax.fori_loop(0, rows // per, piece, (start, start), unroll=True)
     for m in range(2):
         cols_ref[:, m, :] = jnp.broadcast_to(jnp.max(most[m], axis=0, keepdims=True), (cols_ref.shape[0], HD))
         for block in range(0, rows, HD):
@@ -227,33 +227,62 @@
             rows_ref[m : m + 1, block : block + count] = turned[:, :count]
 
 
-def cot_kernel(at_ref, near_ref, far_ref, *refs):
-    weights, out_refs = refs[:4], refs[4:]
-    x, core = at_ref[0], at_ref[3]
+def cot_terms(c_is_own, own, other, own_spill, other_spill, wide):
     dims = (((0,), (0,)), ((), ()))
-    groups, _, seq = near_ref.shape
+    seq = own.shape[2]
     total = None
-    extra_cot, extra_weight = [], []
-    for back, weight in enumerate(weights):
-        at_x = x - back
-        at_x = jnp.where(at_x < 0, at_x + len(weights), at_x)
+    for c in range(2):
+        cot = jnp.where(c_is_own[c], own, other).reshape(2 * HD, seq)
+        start = 2 * c * HD
+        term = lax.dot_general(cot, wide[start : start + 2 * HD], dims, preferred_element_type=full)
+        total = term if total is None else total + term
+    cot = jnp.where(c_is_own[0], own_spill, other_spill)
+    return total + lax.dot_general(cot, wide[4 * HD :], dims, preferred_element_type=full)
+
+
+def placed_back(x, back, count):
+    at_x = x - back
+    return jnp.where(at_x < 0, at_x + count, at_x)
+
+
+def cot_first_kernel(at_ref, near_ref, far_ref, *refs):
+    weights, out_ref = refs[:3], refs[3]
+    core = at_ref[3]
+    groups = near_ref.shape[0]
+    total = None
+    for back, weight in zip((0, 1, 3), weights):
+        at_x = placed_back(at_ref[0], back, groups // 2)
         wide = jnp.concatenate([weight[h] for h in range(4)], axis=1)
-        for c in range(2):
-            own, other = near_ref[pl.ds(2 * at_x, 2)], far_ref[pl.ds(2 * at_x, 2)]
-            cot = jnp.where(core == c, own, other).reshape(2 * HD, seq)
-            start = 2 * c * HD
-            term = lax.dot_general(cot, wide[start : start + 2 * HD], dims, preferred_element_type=full)
-            total = term if total is None else total + term
         y = jnp.minimum(2 * at_x + 2, groups - 1)
-        extra_cot.append(jnp.where(core == 0, near_ref[y, :SPILL, :], far_ref[y, :SPILL, :]))
-        extra_weight.append(wide[4 * HD :])
-    extra_cot, extra_weight = jnp.concatenate(extra_cot, axis=0), jnp.concatenate(extra_weight, axis=0)
-    total = total + lax.dot_general(extra_cot, extra_weight, dims, preferred_element_type=full)
-    total = total.astype(half)
-    out_refs[0][...] = total[:, :HD]
-    out_refs[1][...] = total[:, HD : 2 * HD]
-    out_refs[2][0] = total[:, 2 * HD : 3 * HD]
-    out_refs[2][1] = total[:, 3 * HD :]
+        pair = pl.ds(2 * at_x, 2)
+        term = cot_terms(
+            (core == 0, core == 1), near_ref[pair], far_ref[pair], near_ref[y, :SPILL], far_ref[y, :SPILL], wide
+        )
+        total = term if total is None else total + term
+    out_ref[...] = total
+
+
+def cot_last_kernel(at_ref, weight_ref, near_ref, far_ref, first_ref, *refs):
+    own_ref, one_ref, two_ref, pairs, spills, first, sems = refs
+    core = at_ref[3]
+    groups = near_ref.shape[0]
+    at_x = placed_back(at_ref[0], 2, groups // 2)
+    y = jnp.minimum(2 * at_x + 2, groups - 1)
+    copies = [pltpu.make_async_copy(first_ref, first, sems.at[4])]
+    for k, ref in enumerate((near_ref, far_ref)):
+        copies.append(pltpu.make_async_copy(ref.at[pl.ds(2 * at_x, 2)], pairs.at[k], sems.at[2 * k]))
+        copies.append(pltpu.make_async_copy(ref.at[y, :SPILL], spills.at[k], sems.at[2 * k + 1]))
+    for copy in copies:
+        copy.start()
+    wide = jnp.concatenate([weight_ref[h] for h in range(4)], axis=1)
+    for copy in copies:
+        copy.wait()
+    total = cot_terms((core == 0, core == 1), pairs[0], pairs[1], spills[0], spills[1], wide)
+    total = (first[...] + total).astype(half)
+    own_ref[...] = total[:, :HD]
+    one_ref[...] = total[:, HD : 2 * HD]
+    two_ref[0] = total[:, 2 * HD : 3 * HD]
+    two_ref[1] = total[:, 3 * HD :]
 
 
 def step(
@@ -381,13 +410,22 @@
     )
     before = shifted(part, "x", 1)
     after = shifted(part, "x", 3)
-    parts = [part, before, shifted(before, "x", 1), after]
+    beyond = shifted(before, "x", 1)
+    cot = kernel(cot_first_kernel, (near, far, part, before, after), pltpu.HBM((seq, zls * HD), full), 600000000, 16)
     own, one, two = kernel(
-        cot_kernel,
-        (near, far, *parts),
+        cot_last_kernel,
+        (beyond, in_hbm(near), in_hbm(far), in_hbm(cot)),
         (shape((seq, HD), half), shape((seq, HD), half), shape((2, seq, HD), half)),
-        800000000,
-        16,
+        200000000,
+        12,
+        [
+            pltpu.VMEM((2, 2, HD, seq), half),
+            pltpu.VMEM((2, SPILL, seq), half),
+            pltpu.VMEM((seq, zls * HD), full),
+            pltpu.SemaphoreType.DMA((5,)),
+        ],
+        vmem,
+        [vmem] + [hbm] * 3,
     )
     came = swapped(two, "zl", 2)
     mid = summed([one, came[1]]).astype(half)

time: 216 us -> 244 us (1.13)
  waiting for transfers between devices: 94.6 us -> 122 us
    ppermute x6, waiting for transfers between devices: 34.5 us -> 51.6 us  [shifted(): lax.ppermute(block, axis, [(k, (k + distance) % size) for k in range(size)])]
    ppermute x6, starting transfers between devices: 28.8 us -> 19.7 us  [shifted(): lax.ppermute(block, axis, [(k, (k + distance) % size) for k in range(size)])]
    all_to_all x5, waiting for transfers between devices: 36.9 us -> 45.5 us  [all_to_all(): return lax.all_to_all(blocks, axes, split_axis=0, concat_axis=0, tiled=True)]
    ppermute x6, starting transfers between devices: 25.8 us -> 32.5 us  [swapped(): return lax.ppermute(block, axis, [(k, k ^ bit) for k in range(size)])]
    all_to_all x5, starting transfers between devices: 36.8 us -> 41.3 us  [all_to_all(): return lax.all_to_all(blocks, axes, split_axis=0, concat_axis=0, tiled=True)]
    pallas_call x6 -> x7, Pallas kernels: 12 us -> 13.9 us  [kernel(): pl.pallas_call(body, out_shape=outs, in_specs=[smem] + (spaces or [vmem]...]
  transfers between devices with their start and end apart: 17 -> 17, of which waited for: 11 -> 13; matrix products, arithmetic and copies ran while one was open for 4% -> 3% of each run, Pallas kernels for 4% -> 4%
where the time goes in v1:
time: 244 us; the launch traced here: 243 us
  waiting for transfers between devices  122 us (50%)
  starting transfers between devices  93.5 us (38%)
  Pallas kernels  14.9 us (6%)
  matrix products  3.59 us (1%)
  other arithmetic  3.38 us (1%)
  local copies, waits for them, and re-layouts  2.56 us (1%)
    ppermute x6, waiting for transfers between devices, shifted(): lax.ppermute(block, axis, [(k, (k + distance) % size) for k in range(size)])  51.6 us
    all_to_all x5, waiting for transfers between devices, all_to_all(): return lax.all_to_all(blocks, axes, split_axis=0, concat_axis=0, tiled=True)  45.5 us
    all_to_all x5, starting transfers between devices, all_to_all(): return lax.all_to_all(blocks, axes, split_axis=0, concat_axis=0, tiled=True)  41.3 us
    ppermute x6, starting transfers between devices, swapped(): return lax.ppermute(block, axis, [(k, k ^ bit) for k in range(size)])  32.5 us
    ppermute x6, waiting for transfers between devices, swapped(): return lax.ppermute(block, axis, [(k, k ^ bit) for k in range(size)])  25 us
    ppermute x6, starting transfers between devices, shifted(): lax.ppermute(block, axis, [(k, (k + distance) % size) for k in range(size)])  19.7 us
    pallas_call x7, Pallas kernels, kernel(): pl.pallas_call(body, out_shape=outs, in_specs=[smem] + (spaces or [vmem]...  13.9 us
  transfers between devices with their start and end apart: 17, of which 13 were waited for; matrix products, arithmetic and copies ran while one was open for 3% of the time, Pallas kernels for 4%

profile of v1, /device:TPU:2, one launch (start us, length us, event | category | flops | bytes accessed | tf_op | source)
XLA Modules:
  0.0 242.9 jit_solution(9645126365344020460)
XLA Ops:
  2.6 7.1 %all-to-all-start = ((bf16[8,128,384]{2,1,0:T(8,128)(2,1)}), bf16[8,128,384]{2,1,0:T(8,128)(2,1)S(1)}, u32[]{:S(2)}, u32[]{:S(2)}) async-start(bf16[8,128,384]{2,1,0:T(8,128)(2,1)} %shard_map.172), calls=%async_computation | async-start | bytes 1572864 | tf_op jit(solution)/shard_map/all_to_all | solution.py:48
  10.1 22.7 %all-to-all-done.near_ref = bf16[8,128,384]{2,1,0:T(8,128)(2,1)S(1)} async-done(((bf16[8,128,384]{2,1,0:T(8,128)(2,1)}), bf16[8,128,384]{2,1,0:T(8,128)(2,1)S(1)}, u32[]{:S(2)}, u32[]{:S(2)}) %all-to-all-start) | async-done | bytes 786464 | tf_op jit(solution)/shard_map/all_to_all | solution.py:48
  36.2 6.1 %collective-permute-start.7 = (bf16[384,128]{1,0:T(8,128)(2,1)S(1)}, bf16[384,128]{1,0:T(8,128)(2,1)S(1)}, u32[]{:S(2)}, u32[]{:S(2)}) collective-permute-start(bf16[384,128]{1,0:T(8,128)(2,1)S(1)} %convolution_convert_fusion.att_ref), channel_id=1, source_target_pairs={{0,4},{2,6},{4,0},{6,2},{1,5},{3,7},{5,1},{7,3},{8,12},{10,14},{12... | collective-permute-start | bytes 294920 | tf_op jit(solution)/shard_map/ppermute | solution.py:37
  42.3 5.5 %collective-permute-done.7.came_ref = bf16[384,128]{1,0:T(8,128)(2,1)S(1)} collective-permute-done((bf16[384,128]{1,0:T(8,128)(2,1)S(1)}, bf16[384,128]{1,0:T(8,128)(2,1)S(1)}, u32[]{:S(2)}, u32[]{:S(2)}) %collective-permute-start.7) | collective-permute-done | bytes 98336 | tf_op jit(solution)/shard_map/ppermute | solution.py:37
  50.6 5.0 %collective-permute-done.8.last_ref = bf16[2,384,128]{2,1,0:T(8,128)(2,1)S(1)} collective-permute-done((bf16[2,384,128]{2,1,0:T(8,128)(2,1)S(1)}, bf16[2,384,128]{2,1,0:T(8,128)(2,1)S(1)}, u32[]{:S(2)}, u32[]{:S(2)}) %collective-permute-start.8) | collective-permute-done | bytes 196640 | tf_op jit(solution)/shard_map/ppermute | solution.py:37
  58.3 5.0 %all-to-all-start.1 = ((bf16[4,560,512]{2,1,0:T(8,128)(2,1)}), bf16[4,560,512]{2,1,0:T(8,128)(2,1)S(1)}, u32[]{:S(2)}, u32[]{:S(2)}) async-start(bf16[4,560,512]{2,1,0:T(8,128)(2,1)} %get-tuple-element.34), calls=%async_computation.1 | async-start | bytes 4587520 | tf_op jit(solution)/shard_map/all_to_all | solution.py:48
  64.5 5.3 %collective-permute-start = (bf16[2,256,128]{2,1,0:T(8,128)(2,1)S(1)}, bf16[2,256,128]{2,1,0:T(8,128)(2,1)S(1)}, u32[]{:S(2)}, u32[]{:S(2)}) collective-permute-start(bf16[2,256,128]{2,1,0:T(8,128)(2,1)S(1)} %get-tuple-element.27), channel_id=1, source_target_pairs={{0,4},{2,6},{4,0},{6,2},{1,5},{3,7},{5,1},{7,3},{8,12},{10,14},{12... | collective-permute-start | bytes 393224 | tf_op jit(solution)/shard_map/ppermute | solution.py:37
  69.8 5.4 %collective-permute-done = bf16[2,256,128]{2,1,0:T(8,128)(2,1)S(1)} collective-permute-done((bf16[2,256,128]{2,1,0:T(8,128)(2,1)S(1)}, bf16[2,256,128]{2,1,0:T(8,128)(2,1)S(1)}, u32[]{:S(2)}, u32[]{:S(2)}) %collective-permute-start) | collective-permute-done | bytes 131104 | tf_op jit(solution)/shard_map/ppermute | solution.py:37
  77.9 4.2 %collective-permute-done.1 = bf16[2,256,128]{2,1,0:T(8,128)(2,1)S(1)} collective-permute-done((bf16[2,256,128]{2,1,0:T(8,128)(2,1)S(1)}, bf16[2,256,128]{2,1,0:T(8,128)(2,1)S(1)}, u32[]{:S(2)}, u32[]{:S(2)}) %collective-permute-start.1) | collective-permute-done | bytes 131104 | tf_op jit(solution)/shard_map/ppermute | solution.py:37
  82.1 6.7 %all-to-all-done.1.got_ref = bf16[4,560,512]{2,1,0:T(8,128)(2,1)S(1)} async-done(((bf16[4,560,512]{2,1,0:T(8,128)(2,1)}), bf16[4,560,512]{2,1,0:T(8,128)(2,1)S(1)}, u32[]{:S(2)}, u32[]{:S(2)}) %all-to-all-start.1) | async-done | bytes 2293792 | tf_op jit(solution)/shard_map/all_to_all | solution.py:48
  90.8 14.9 %all-to-all-start.2 = ((bf16[12,256,128]{2,1,0:T(8,128)(2,1)}), bf16[12,256,128]{2,1,0:T(8,128)(2,1)S(1)}, u32[]{:S(2)}, u32[]{:S(2)}) async-start(bf16[12,256,128]{2,1,0:T(8,128)(2,1)} %shard_map.176), calls=%async_computation.2 | async-start | bytes 1572864 | tf_op jit(solution)/shard_map/all_to_all | solution.py:48
  105.8 7.8 %collective-permute-start.2 = (bf16[4,256,128]{2,1,0:T(8,128)(2,1)S(1)}, bf16[4,256,128]{2,1,0:T(8,128)(2,1)S(1)}, u32[]{:S(2)}, u32[]{:S(2)}) collective-permute-start(bf16[4,256,128]{2,1,0:T(8,128)(2,1)S(1)} %pad_maximum_fusion.refs_0_), channel_id=1, source_target_pairs={{0,64},{64,128},{128,0},{1,65},{65,129},{129,1},{2,66},{66,130},{1... | collective-permute-start | bytes 786440 | tf_op jit(solution)/shard_map/ppermute | solution.py:32
  115.5 31.8 %collective-permute-done.2.refs_1_ = bf16[4,256,128]{2,1,0:T(8,128)(2,1)S(1)} collective-permute-done((bf16[4,256,128]{2,1,0:T(8,128)(2,1)S(1)}, bf16[4,256,128]{2,1,0:T(8,128)(2,1)S(1)}, u32[]{:S(2)}, u32[]{:S(2)}) %collective-permute-start.2) | collective-permute-done | bytes 262176 | tf_op jit(solution)/shard_map/ppermute | solution.py:32
  152.4 3.9 %collective-permute-start.9 = (bf16[4,560,128]{2,1,0:T(8,128)(2,1)S(1)}, bf16[4,560,128]{2,1,0:T(8,128)(2,1)S(1)}, u32[]{:S(2)}, u32[]{:S(2)}) collective-permute-start(bf16[4,560,128]{2,1,0:T(8,128)(2,1)S(1)} %shard_map.171.refs_0_), channel_id=1, source_target_pairs={{0,576},{192,0},{384,192},{576,384},{1,577},{193,1},{385,193},{577... | collective-permute-start | bytes 1720328 | tf_op jit(solution)/shard_map/ppermute | solution.py:32
  156.2 8.2 %collective-permute-done.4.refs_1_ = bf16[4,560,128]{2,1,0:T(8,128)(2,1)S(1)} collective-permute-done((bf16[4,560,128]{2,1,0:T(8,128)(2,1)S(1)}, bf16[4,560,128]{2,1,0:T(8,128)(2,1)S(1)}, u32[]{:S(2)}, u32[]{:S(2)}) %collective-permute-start.4) | collective-permute-done | bytes 573472 | tf_op jit(solution)/shard_map/ppermute | solution.py:32
  169.4 9.3 %collective-permute-done.5.weight_ref = bf16[4,560,128]{2,1,0:T(8,128)(2,1)S(1)} collective-permute-done((bf16[4,560,128]{2,1,0:T(8,128)(2,1)S(1)}, bf16[4,560,128]{2,1,0:T(8,128)(2,1)S(1)}, u32[]{:S(2)}, u32[]{:S(2)}) %collective-permute-start.5) | collective-permute-done | bytes 573472 | tf_op jit(solution)/shard_map/ppermute | solution.py:32
  181.0 9.7 %collective-permute-start.10 = (bf16[2,384,128]{2,1,0:T(8,128)(2,1)S(1)}, bf16[2,384,128]{2,1,0:T(8,128)(2,1)S(1)}, u32[]{:S(2)}, u32[]{:S(2)}) collective-permute-start(bf16[2,384,128]{2,1,0:T(8,128)(2,1)S(1)} %get-tuple-element.32), channel_id=1, source_target_pairs={{0,4},{2,6},{4,0},{6,2},{1,5},{3,7},{5,1},{7,3},{8,12},{10,14},{12... | collective-permute-start | bytes 589832 | tf_op jit(solution)/shard_map/ppermute | solution.py:37
  191.7 4.8 %collective-permute-done.10 = bf16[2,384,128]{2,1,0:T(8,128)(2,1)S(1)} collective-permute-done((bf16[2,384,128]{2,1,0:T(8,128)(2,1)S(1)}, bf16[2,384,128]{2,1,0:T(8,128)(2,1)S(1)}, u32[]{:S(2)}, u32[]{:S(2)}) %collective-permute-start.10) | collective-permute-done | bytes 196640 | tf_op jit(solution)/shard_map/ppermute | solution.py:37
  196.5 6.1 %collective-permute-start.11 = (bf16[384,128]{1,0:T(8,128)(2,1)S(1)}, bf16[384,128]{1,0:T(8,128)(2,1)S(1)}, u32[]{:S(2)}, u32[]{:S(2)}) collective-permute-start(bf16[384,128]{1,0:T(8,128)(2,1)S(1)} %fusion.11), channel_id=1, source_target_pairs={{0,2},{2,0},{4,6},{6,4},{1,3},{3,1},{5,7},{7,5},{8,10},{10,8},{12,... | collective-permute-start | bytes 294920 | tf_op jit(solution)/shard_map/ppermute | solution.py:37
  203.6 3.0 %shard_map.177 = (f32[688,128]{1,0:T(8,128)}, f32[688,128]{1,0:T(8,128)}, f32[688,128]{1,0:T(8,128)}, f32[2,688]{1,0:T(2,128)S(1)}, f32[12,2,128]{2,1,0:T(2,128)}) custom-call(s32[5]{0:T(128)S(1)} %stack.40.at_ref, bf16[12,256,128]{2,1,0:T(8,128)(2,1)S(1)} %all-to-all-done.2.got_ref, f32[688,128]{1,0:T(8,128)} %multiply_multiply_fusion.1.refs_0_, ...), custom_call_target="tpu_custom_call" | custom-call | flops 10000000 | bytes 3000000 | tf_op jit(solution)/shard_map/pallas_call | solution.py:312
  206.6 10.4 %all-to-all-start.4 = ((f32[12,2,128]{2,1,0:T(2,128)}), f32[12,2,128]{2,1,0:T(2,128)S(1)}, u32[]{:S(2)}, u32[]{:S(2)}) async-start(f32[12,2,128]{2,1,0:T(2,128)} %get-tuple-element.38), calls=%async_computation.4 | async-start | bytes 24576 | tf_op jit(solution)/shard_map/all_to_all | solution.py:48
  218.8 6.9 %all-to-all-done.4 = f32[12,2,128]{2,1,0:T(2,128)S(1)} async-done(((f32[12,2,128]{2,1,0:T(2,128)}), f32[12,2,128]{2,1,0:T(2,128)S(1)}, u32[]{:S(2)}, u32[]{:S(2)}) %all-to-all-start.4) | async-done | bytes 12320 | tf_op jit(solution)/shard_map/all_to_all | solution.py:48
  226.4 3.9 %all-to-all-start.3 = ((f32[32,2,688]{2,1,0:T(2,128)}), f32[32,2,688]{2,1,0:T(2,128)S(1)}, u32[]{:S(2)}, u32[]{:S(2)}) async-start(f32[32,2,688]{2,1,0:T(2,128)} %broadcast_in_dim.7), calls=%async_computation.3 | async-start | bytes 393216 | tf_op jit(solution)/shard_map/all_to_all | solution.py:48
  232.6 9.2 %all-to-all-done.3 = f32[32,2,688]{2,1,0:T(2,128)S(1)} async-done(((f32[32,2,688]{2,1,0:T(2,128)}), f32[32,2,688]{2,1,0:T(2,128)S(1)}, u32[]{:S(2)}, u32[]{:S(2)}) %all-to-all-start.3) | async-done | bytes 176160 | tf_op jit(solution)/shard_map/all_to_all | solution.py:48
  (89 shorter events, 38.9 us)
Async XLA Ops:
  2.6 30.2 %all-to-all-start = ((bf16[8,128,384]{2,1,0:T(8,128)(2,1)}), bf16[8,128,384]{2,1,0:T(8,128)(2,1)S(1)}, u32[]{:S(2)}, u32[]{:S(2)}) async-start(bf16[8,128,384]{2,1,0:T(8,128)(2,1)} %shard_map.172), calls=%async_computation | async-start | bytes 1572864 | tf_op jit(solution)/shard_map/all_to_all | solution.py:48
  32.9 22.8 %collective-permute-start.6 = (bf16[8,128,384]{2,1,0:T(8,128)(2,1)S(1)}, bf16[8,128,384]{2,1,0:T(8,128)(2,1)S(1)}, u32[]{:S(2)}, u32[]{:S(2)}) collective-permute-start(bf16[8,128,384]{2,1,0:T(8,128)(2,1)S(1)} %all-to-all-done.near_ref), channel_id=1, source_target_pairs={{0,1},{1,0},{2,3},{3,2},{4,5},{5,4},{6,7},{7,6},{8,9},{9,8},{10,11... | collective-permute-start | bytes 2359304 | tf_op jit(solution)/shard_map/ppermute | solution.py:32
  36.2 11.6 %collective-permute-start.7 = (bf16[384,128]{1,0:T(8,128)(2,1)S(1)}, bf16[384,128]{1,0:T(8,128)(2,1)S(1)}, u32[]{:S(2)}, u32[]{:S(2)}) collective-permute-start(bf16[384,128]{1,0:T(8,128)(2,1)S(1)} %convolution_convert_fusion.att_ref), channel_id=1, source_target_pairs={{0,4},{2,6},{4,0},{6,2},{1,5},{3,7},{5,1},{7,3},{8,12},{10,14},{12... | collective-permute-start | bytes 294920 | tf_op jit(solution)/shard_map/ppermute | solution.py:37
  47.9 7.8 %collective-permute-start.8 = (bf16[2,384,128]{2,1,0:T(8,128)(2,1)S(1)}, bf16[2,384,128]{2,1,0:T(8,128)(2,1)S(1)}, u32[]{:S(2)}, u32[]{:S(2)}) collective-permute-start(bf16[2,384,128]{2,1,0:T(8,128)(2,1)S(1)} %pad_maximum_fusion.1), channel_id=1, source_target_pairs={{0,2},{2,0},{4,6},{6,4},{1,3},{3,1},{5,7},{7,5},{8,10},{10,8},{12,... | collective-permute-start | bytes 589832 | tf_op jit(solution)/shard_map/ppermute | solution.py:37
  58.3 30.6 %all-to-all-start.1 = ((bf16[4,560,512]{2,1,0:T(8,128)(2,1)}), bf16[4,560,512]{2,1,0:T(8,128)(2,1)S(1)}, u32[]{:S(2)}, u32[]{:S(2)}) async-start(bf16[4,560,512]{2,1,0:T(8,128)(2,1)} %get-tuple-element.34), calls=%async_computation.1 | async-start | bytes 4587520 | tf_op jit(solution)/shard_map/all_to_all | solution.py:48
  64.5 10.7 %collective-permute-start = (bf16[2,256,128]{2,1,0:T(8,128)(2,1)S(1)}, bf16[2,256,128]{2,1,0:T(8,128)(2,1)S(1)}, u32[]{:S(2)}, u32[]{:S(2)}) collective-permute-start(bf16[2,256,128]{2,1,0:T(8,128)(2,1)S(1)} %get-tuple-element.27), channel_id=1, source_target_pairs={{0,4},{2,6},{4,0},{6,2},{1,5},{3,7},{5,1},{7,3},{8,12},{10,14},{12... | collective-permute-start | bytes 393224 | tf_op jit(solution)/shard_map/ppermute | solution.py:37
  75.3 6.9 %collective-permute-start.1 = (bf16[2,256,128]{2,1,0:T(8,128)(2,1)S(1)}, bf16[2,256,128]{2,1,0:T(8,128)(2,1)S(1)}, u32[]{:S(2)}, u32[]{:S(2)}) collective-permute-start(bf16[2,256,128]{2,1,0:T(8,128)(2,1)S(1)} %pad_maximum_fusion.2), channel_id=1, source_target_pairs={{0,2},{2,0},{4,6},{6,4},{1,3},{3,1},{5,7},{7,5},{8,10},{10,8},{12,... | collective-permute-start | bytes 393224 | tf_op jit(solution)/shard_map/ppermute | solution.py:37
  90.8 76.0 %copy-start.1 = (bf16[8,128,384]{2,1,0:T(8,128)(2,1)S(1)}, bf16[8,128,384]{2,1,0:T(8,128)(2,1)}, u32[]{:S(2)}) copy-start(bf16[8,128,384]{2,1,0:T(8,128)(2,1)} %get-tuple-element.29.near_ref) | copy-start | bytes 2359300
  90.8 76.0 %copy-start.2 = (bf16[8,128,384]{2,1,0:T(8,128)(2,1)S(1)}, bf16[8,128,384]{2,1,0:T(8,128)(2,1)}, u32[]{:S(2)}) copy-start(bf16[8,128,384]{2,1,0:T(8,128)(2,1)} %get-tuple-element.30.far_ref) | copy-start | bytes 2359300
  90.8 112.8 %all-to-all-start.2 = ((bf16[12,256,128]{2,1,0:T(8,128)(2,1)}), bf16[12,256,128]{2,1,0:T(8,128)(2,1)S(1)}, u32[]{:S(2)}, u32[]{:S(2)}) async-start(bf16[12,256,128]{2,1,0:T(8,128)(2,1)} %shard_map.176), calls=%async_computation.2 | async-start | bytes 1572864 | tf_op jit(solution)/shard_map/all_to_all | solution.py:48
  105.8 41.5 %collective-permute-start.2 = (bf16[4,256,128]{2,1,0:T(8,128)(2,1)S(1)}, bf16[4,256,128]{2,1,0:T(8,128)(2,1)S(1)}, u32[]{:S(2)}, u32[]{:S(2)}) collective-permute-start(bf16[4,256,128]{2,1,0:T(8,128)(2,1)S(1)} %pad_maximum_fusion.refs_0_), channel_id=1, source_target_pairs={{0,64},{64,128},{128,0},{1,65},{65,129},{129,1},{2,66},{66,130},{1... | collective-permute-start | bytes 786440 | tf_op jit(solution)/shard_map/ppermute | solution.py:32
  113.6 36.0 %collective-permute-start.3 = (bf16[4,256,128]{2,1,0:T(8,128)(2,1)S(1)}, bf16[4,256,128]{2,1,0:T(8,128)(2,1)S(1)}, u32[]{:S(2)}, u32[]{:S(2)}) collective-permute-start(bf16[4,256,128]{2,1,0:T(8,128)(2,1)S(1)} %pad_maximum_fusion.refs_0_), channel_id=1, source_target_pairs={{0,128},{64,0},{128,64},{1,129},{65,1},{129,65},{2,130},{66,2},{13... | collective-permute-start | bytes 786440 | tf_op jit(solution)/shard_map/ppermute | solution.py:32
  150.4 14.1 %collective-permute-start.4 = (bf16[4,560,128]{2,1,0:T(8,128)(2,1)S(1)}, bf16[4,560,128]{2,1,0:T(8,128)(2,1)S(1)}, u32[]{:S(2)}, u32[]{:S(2)}) collective-permute-start(bf16[4,560,128]{2,1,0:T(8,128)(2,1)S(1)} %shard_map.171.refs_0_), channel_id=1, source_target_pairs={{0,192},{192,384},{384,576},{576,0},{1,193},{193,385},{385,577},{5... | collective-permute-start | bytes 1720328 | tf_op jit(solution)/shard_map/ppermute | solution.py:32
  152.4 14.3 %collective-permute-start.9 = (bf16[4,560,128]{2,1,0:T(8,128)(2,1)S(1)}, bf16[4,560,128]{2,1,0:T(8,128)(2,1)S(1)}, u32[]{:S(2)}, u32[]{:S(2)}) collective-permute-start(bf16[4,560,128]{2,1,0:T(8,128)(2,1)S(1)} %shard_map.171.refs_0_), channel_id=1, source_target_pairs={{0,576},{192,0},{384,192},{576,384},{1,577},{193,1},{385,193},{577... | collective-permute-start | bytes 1720328 | tf_op jit(solution)/shard_map/ppermute | solution.py:32
  164.5 14.2 %collective-permute-start.5 = (bf16[4,560,128]{2,1,0:T(8,128)(2,1)S(1)}, bf16[4,560,128]{2,1,0:T(8,128)(2,1)S(1)}, u32[]{:S(2)}, u32[]{:S(2)}) collective-permute-start(bf16[4,560,128]{2,1,0:T(8,128)(2,1)S(1)} %collective-permute-done.4.refs_1_), channel_id=1, source_target_pairs={{0,192},{192,384},{384,576},{576,0},{1,193},{193,385},{385,577},{5... | collective-permute-start | bytes 1720328 | tf_op jit(solution)/shard_map/ppermute | solution.py:32
  169.3 33.3 %copy-start.18 = (f32[688]{0:T(1024)S(1)}, f32[688]{0:T(1024)}, u32[]{:S(2)}) copy-start(f32[688]{0:T(1024)} %param.17) | copy-start | bytes 8260
  181.0 49.3 %copy-start.5 = (bf16[384,128]{1,0:T(8,128)(2,1)S(1)}, bf16[384,128]{1,0:T(8,128)(2,1)}, u32[]{:S(2)}) copy-start(bf16[384,128]{1,0:T(8,128)(2,1)} %copy-done.4) | copy-start | bytes 294916
  181.0 49.5 %copy-start.10 = (f32[384,384]{0,1:T(8,128)S(1)}, f32[384,384]{0,1:T(8,128)}, u32[]{:S(2)}) copy-start(f32[384,384]{0,1:T(8,128)} %copy-done.9) | copy-start | bytes 1769476
  181.0 15.5 %collective-permute-start.10 = (bf16[2,384,128]{2,1,0:T(8,128)(2,1)S(1)}, bf16[2,384,128]{2,1,0:T(8,128)(2,1)S(1)}, u32[]{:S(2)}, u32[]{:S(2)}) collective-permute-start(bf16[2,384,128]{2,1,0:T(8,128)(2,1)S(1)} %get-tuple-element.32), channel_id=1, source_target_pairs={{0,4},{2,6},{4,0},{6,2},{1,5},{3,7},{5,1},{7,3},{8,12},{10,14},{12... | collective-permute-start | bytes 589832 | tf_op jit(solution)/shard_map/ppermute | solution.py:37
  196.5 33.8 %collective-permute-start.11 = (bf16[384,128]{1,0:T(8,128)(2,1)S(1)}, bf16[384,128]{1,0:T(8,128)(2,1)S(1)}, u32[]{:S(2)}, u32[]{:S(2)}) collective-permute-start(bf16[384,128]{1,0:T(8,128)(2,1)S(1)} %fusion.11), channel_id=1, source_target_pairs={{0,2},{2,0},{4,6},{6,4},{1,3},{3,1},{5,7},{7,5},{8,10},{10,8},{12,... | collective-permute-start | bytes 294920 | tf_op jit(solution)/shard_map/ppermute | solution.py:37
  206.6 35.3 %copy-start.11 = (f32[688,128]{1,0:T(8,128)S(1)}, f32[688,128]{1,0:T(8,128)}, u32[]{:S(2)}) copy-start(f32[688,128]{1,0:T(8,128)} %get-tuple-element.36) | copy-start | bytes 1056772
  206.6 35.3 %copy-start.12 = (f32[688,128]{1,0:T(8,128)S(1)}, f32[688,128]{1,0:T(8,128)}, u32[]{:S(2)}) copy-start(f32[688,128]{1,0:T(8,128)} %get-tuple-element.39) | copy-start | bytes 1056772
  206.6 19.1 %all-to-all-start.4 = ((f32[12,2,128]{2,1,0:T(2,128)}), f32[12,2,128]{2,1,0:T(2,128)S(1)}, u32[]{:S(2)}, u32[]{:S(2)}) async-start(f32[12,2,128]{2,1,0:T(2,128)} %get-tuple-element.38), calls=%async_computation.4 | async-start | bytes 24576 | tf_op jit(solution)/shard_map/all_to_all | solution.py:48
  226.4 15.3 %all-to-all-start.3 = ((f32[32,2,688]{2,1,0:T(2,128)}), f32[32,2,688]{2,1,0:T(2,128)S(1)}, u32[]{:S(2)}, u32[]{:S(2)}) async-start(f32[32,2,688]{2,1,0:T(2,128)} %broadcast_in_dim.7), calls=%async_computation.3 | async-start | bytes 393216 | tf_op jit(solution)/shard_map/all_to_all | solution.py:48
  (17 other events, 236.3 us)

commit v2 on v1

--- a/solution.py
+++ b/solution.py
@@ -25,6 +25,7 @@
 half = jnp.bfloat16
 full = jnp.float32
 SPILL = 48
+EXTRA = 16
 
 
 def shifted(block, axis, distance):
@@ -119,51 +120,74 @@
         out_ref[k] = turned
 
 
-def out_kernel(at_ref, near_ref, far_ref, att_ref, came_ref, last_ref, out_ref, near_kept, far_kept, scratch, sems):
-    core = at_ref[3]
+def out_kernel(side, at_ref, part_ref, att_ref, came_ref, last_ref, *refs):
+    out_ref, kept_ref, scratch, firsts, sems = refs[-5:]
+    zl, core = at_ref[2], at_ref[3]
+    c = core if side == 0 else 1 - core
+    spilling = jnp.logical_and(zl == 0, c == 0)
     att = jnp.concatenate([att_ref[...], last_ref[0], came_ref[...], last_ref[1]], axis=1)
-    places = out_ref.shape[0]
-    scratch[places - 1, 4 * HD :, :] = jnp.zeros((SPILL, out_ref.shape[2]), half)
-    copies = [
-        pltpu.make_async_copy(near_ref, near_kept, sems.at[places]),
-        pltpu.make_async_copy(far_ref, far_kept, sems.at[places + 1]),
-    ]
+    groups = part_ref.shape[0]
+    places = groups // 2
+    copies = [pltpu.make_async_copy(part_ref, kept_ref, sems.at[groups])]
+    if side == 1:
+        scratch[groups, :EXTRA, :] = jnp.zeros((EXTRA, out_ref.shape[2]), half)
+        copies.append(
+            pltpu.make_async_copy(
+                scratch.at[groups, :EXTRA], out_ref.at[places - 1, 4 * HD :], sems.at[groups + places]
+            )
+        )
     for copy in copies:
         copy.start()
-
-    def put(part, c, k):
-        whole = jnp.dot(part[2 * k : 2 * k + 2].reshape(2 * HD, -1), att, preferred_element_type=full)
-        whole = whole.astype(half)
+    for k in range(places - 1, -1, -1):
+        whole = jnp.dot(part_ref[2 * k : 2 * k + 2].reshape(2 * HD, -1), att, preferred_element_type=full).astype(half)
+        scratch[2 * k : 2 * k + 2] = whole.reshape(2, HD, -1)
+        firsts[k] = whole[:SPILL]
+        if 0 < k < places - 1:
+            rows = k * EXTRA
+            scratch[2 * k, :rows, :] = jnp.where(spilling, firsts[k + 1, :rows, :], whole[:rows])
         for y in range(2):
             start = pl.multiple_of(y * 2 * HD + c * HD, HD)
-            scratch[k, pl.ds(start, HD), :] = whole[y * HD : (y + 1) * HD]
-
-    for k in range(places - 1, -1, -1):
-        put(near_ref, core, k)
-        put(far_ref, 1 - core, k)
-        if k > 0:
-            scratch[k - 1, 4 * HD :, :] = scratch[k, :SPILL, :]
-        copy = pltpu.make_async_copy(scratch.at[k], out_ref.at[k], sems.at[k])
-        copy.start()
-        copies.append(copy)
+            copy = pltpu.make_async_copy(scratch.at[2 * k + y], out_ref.at[k, pl.ds(start, HD)], sems.at[2 * k + y])
+            copy.start()
+            copies.append(copy)
+
+    @pl.when(c == 0)
+    def _():
+        spills = [
+            pltpu.make_async_copy(
+                firsts.at[k + 1, k * EXTRA : (k + 1) * EXTRA], out_ref.at[k, 4 * HD :], sems.at[groups + 1 + k]
+            )
+            for k in range(places - 1)
+        ]
+        for copy in spills:
+            copy.start()
+        for copy in spills:
+            copy.wait()
+
     for copy in copies:
         copy.wait()
 
 
 def send_kernel(zhs, at_ref, got_ref, out_ref, padded, sems):
     x, zl, rows = at_ref[0], at_ref[2], at_ref[4]
-    sources, count = got_ref.shape[0], got_ref.shape[1]
+    sources, count = got_ref.shape[0], got_ref.shape[1] - EXTRA
     padded[count:, :] = jnp.zeros((padded.shape[0] - count, padded.shape[1]), half)
 
-    def piece(r, carry):
-        place = pl.ds(pl.multiple_of(r * 16, 16), 16)
+    def summed_at(place):
         total = got_ref[0, place, :].astype(full)
         for d in range(1, sources):
             total = total + got_ref[d, place, :].astype(full)
-        padded[place, :] = total.astype(half)
+        return total.astype(half)
+
+    def piece(r, carry):
+        place = pl.ds(pl.multiple_of(r * 16, 16), 16)
+        padded[place, :] = summed_at(place)
         return carry
 
-    lax.fori_loop(0, count // 16, piece, 0, unroll=5)
+    lax.fori_loop(0, count // 16, piece, 0, unroll=4)
+    padded[count : count + SPILL, :] = padded[:SPILL, :]
+    last = pl.ds(pl.multiple_of(count + x * EXTRA, EXTRA), EXTRA)
+    padded[last, :] = summed_at(slice(count, count + EXTRA))
     copies = []
     for z in range(zhs):
         group = jnp.clip(group_of(x * zhs + z, zl, rows) - 2 * x, 0, 2)
@@ -308,13 +332,14 @@
     smem, vmem = pl.BlockSpec(memory_space=pltpu.SMEM), pl.BlockSpec(memory_space=pltpu.VMEM)
     shape = jax.ShapeDtypeStruct
 
-    def kernel(body, arguments, outs, flops, room, scratch=(), space=vmem, spaces=None):
+    def kernel(body, arguments, outs, flops, room, scratch=(), space=vmem, spaces=None, aliases={}):
         return pl.pallas_call(
             body,
             out_shape=outs,
             in_specs=[smem] + (spaces or [vmem] * len(arguments)),
             out_specs=jax.tree.map(lambda _: space, outs),
             scratch_shapes=scratch,
+            input_output_aliases=aliases,
             compiler_params=pltpu.CompilerParams(vmem_limit_bytes=room * 1024 * 1024),
             cost_estimate=pl.CostEstimate(flops=flops, bytes_accessed=3000000, transcendentals=0),
         )(at, *arguments)
@@ -348,16 +373,26 @@
 
     hbm = pl.BlockSpec(memory_space=pltpu.HBM)
     in_hbm = functools.partial(pltpu.with_memory_space_constraint, memory_space=pltpu.HBM)
-    cut = 4 * HD + SPILL
+    cut = 4 * HD + EXTRA
     kept = pltpu.HBM((ys, HD, seq), half)
-    partial, near, far = kernel(
-        out_kernel,
-        (near, far, attended, came, last),
-        (pltpu.HBM((xs, cut, zls * HD), half), kept, kept),
-        800000000,
-        16,
-        [pltpu.VMEM((xs, cut, zls * HD), half), pltpu.SemaphoreType.DMA((xs + 2,))],
+    made = pltpu.HBM((xs, cut, zls * HD), half)
+    room = [
+        pltpu.VMEM((ys + 1, HD, zls * HD), half),
+        pltpu.VMEM((xs, SPILL, zls * HD), half),
+        pltpu.SemaphoreType.DMA((ys + 1 + xs,)),
+    ]
+    att = (attended, came, last)
+    partial, near = kernel(functools.partial(out_kernel, 0), (near, *att), (made, kept), 400000000, 12, room, hbm)
+    partial, far = kernel(
+        functools.partial(out_kernel, 1),
+        (far, *att, partial),
+        (made, kept),
+        400000000,
+        12,
+        room,
         hbm,
+        [vmem] * 4 + [hbm],
+        {5: 0},
     )
     partial = all_to_all(partial, "x")
     partial = kernel(
@@ -390,14 +425,11 @@
     )
     cols_max = jnp.max(all_to_all(cols_max, DP), axis=0)
     rows_max = jnp.max(lax.all_gather(rows_max, "c"), axis=0)
-    rows_max = jnp.broadcast_to(rows_max[None], (ys * zls, *rows_max.shape))
-    rows_max = jnp.max(all_to_all(rows_max, ("y", "zl")), axis=0)
-    next_first_code = (
-        first_new / (jnp.minimum(rows_max[0][:, None], cols_max[0][None, :]) + code_eps)
-    ).astype(half)
-    next_second_code = (
-        second_new / (jnp.minimum(rows_max[1][:, None], cols_max[1][None, :]) + code_eps)
-    ).astype(half)
+    rows_max = jnp.broadcast_to(rows_max.astype(half)[None], (ys * zls, *rows_max.shape))
+    rows_max = all_to_all(rows_max, ("y", "zl"))
+    rows_max = jnp.max(rows_max.astype(full), axis=0)
+    next_first_code = (first_new / (jnp.minimum(rows_max[0][:, None], cols_max[0][None, :]) + code_eps)).astype(half)
+    next_second_code = (second_new / (jnp.minimum(rows_max[1][:, None], cols_max[1][None, :]) + code_eps)).astype(half)
 
     parts = [part] + [shifted(part, "zh", d) for d in range(1, zhs)]
     part = kernel(

time: 244 us -> 223 us (0.914)
  waiting for transfers between devices: 122 us -> 104 us
  starting transfers between devices: 93.5 us -> 87.2 us
    ppermute x6, waiting for transfers between devices: 51.6 us -> 35.2 us  [shifted(): lax.ppermute(block, axis, [(k, (k + distance) % size) for k in range(size)])]
    ppermute x6, starting transfers between devices: 32.5 us -> 21.8 us  [swapped(): return lax.ppermute(block, axis, [(k, k ^ bit) for k in range(size)])]
    all_to_all x5, waiting for transfers between devices: 45.5 us -> 38.2 us  [all_to_all(): return lax.all_to_all(blocks, axes, split_axis=0, concat_axis=0, tiled=True)]
    ppermute x6, starting transfers between devices: 19.7 us -> 25.8 us  [shifted(): lax.ppermute(block, axis, [(k, (k + distance) % size) for k in range(size)])]
    ppermute x6, waiting for transfers between devices: 25 us -> 30.4 us  [swapped(): return lax.ppermute(block, axis, [(k, k ^ bit) for k in range(size)])]
    pallas_call x7 -> x8, Pallas kernels: 13.9 us -> 15.9 us  [kernel(): pl.pallas_call(body, out_shape=outs, in_specs=[smem] + (spaces or [vmem]...]
  transfers between devices with their start and end apart: 17 -> 17, of which waited for: 13 -> 12; matrix products, arithmetic and copies ran while one was open for 3% -> 3% of each run, Pallas kernels for 4% -> 5%
where the time goes in v2:
time: 223 us; the launch traced here: 222 us
  waiting for transfers between devices  104 us (47%)
  starting transfers between devices  87.2 us (39%)
  Pallas kernels  16.9 us (8%)
  other arithmetic  4.5 us (2%)
  local copies, waits for them, and re-layouts  3.66 us (2%)
  matrix products  3.45 us (2%)
    all_to_all x5, starting transfers between devices, all_to_all(): return lax.all_to_all(blocks, axes, split_axis=0, concat_axis=0, tiled=True)  39.6 us
    all_to_all x5, waiting for transfers between devices, all_to_all(): return lax.all_to_all(blocks, axes, split_axis=0, concat_axis=0, tiled=True)  38.2 us
    ppermute x6, waiting for transfers between devices, shifted(): lax.ppermute(block, axis, [(k, (k + distance) % size) for k in range(size)])  35.2 us
    ppermute x6, waiting for transfers between devices, swapped(): return lax.ppermute(block, axis, [(k, k ^ bit) for k in range(size)])  30.4 us
    ppermute x6, starting transfers between devices, shifted(): lax.ppermute(block, axis, [(k, (k + distance) % size) for k in range(size)])  25.8 us
    ppermute x6, starting transfers between devices, swapped(): return lax.ppermute(block, axis, [(k, k ^ bit) for k in range(size)])  21.8 us
    pallas_call x8, Pallas kernels, kernel(): pl.pallas_call(body, out_shape=outs, in_specs=[smem] + (spaces or [vmem]...  15.9 us
  transfers between devices with their start and end apart: 17, of which 12 were waited for; matrix products, arithmetic and copies ran while one was open for 3% of the time, Pallas kernels for 5%

profile of v2, /device:TPU:2, one launch (start us, length us, event | category | flops | bytes accessed | tf_op | source)
XLA Modules:
  0.0 222.4 jit_solution(17974384935871241709)
XLA Ops:
  2.6 7.1 %all-to-all-start = ((bf16[8,128,384]{2,1,0:T(8,128)(2,1)}), bf16[8,128,384]{2,1,0:T(8,128)(2,1)S(1)}, u32[]{:S(2)}, u32[]{:S(2)}) async-start(bf16[8,128,384]{2,1,0:T(8,128)(2,1)} %shard_map.172), calls=%async_computation | async-start | bytes 1572864 | tf_op jit(solution)/shard_map/all_to_all | solution.py:49
  10.1 22.7 %all-to-all-done.part_ref = bf16[8,128,384]{2,1,0:T(8,128)(2,1)S(1)} async-done(((bf16[8,128,384]{2,1,0:T(8,128)(2,1)}), bf16[8,128,384]{2,1,0:T(8,128)(2,1)S(1)}, u32[]{:S(2)}, u32[]{:S(2)}) %all-to-all-start) | async-done | bytes 786464 | tf_op jit(solution)/shard_map/all_to_all | solution.py:49
  36.8 6.1 %collective-permute-start.6 = (bf16[384,128]{1,0:T(8,128)(2,1)S(1)}, bf16[384,128]{1,0:T(8,128)(2,1)S(1)}, u32[]{:S(2)}, u32[]{:S(2)}) collective-permute-start(bf16[384,128]{1,0:T(8,128)(2,1)S(1)} %convolution_convert_fusion.att_ref), channel_id=1, source_target_pairs={{0,4},{2,6},{4,0},{6,2},{1,5},{3,7},{5,1},{7,3},{8,12},{10,14},{12... | collective-permute-start | bytes 294920 | tf_op jit(solution)/shard_map/ppermute | solution.py:38
  42.9 5.5 %collective-permute-done.6.came_ref = bf16[384,128]{1,0:T(8,128)(2,1)S(1)} collective-permute-done((bf16[384,128]{1,0:T(8,128)(2,1)S(1)}, bf16[384,128]{1,0:T(8,128)(2,1)S(1)}, u32[]{:S(2)}, u32[]{:S(2)}) %collective-permute-start.6) | collective-permute-done | bytes 98336 | tf_op jit(solution)/shard_map/ppermute | solution.py:38
  51.3 5.0 %collective-permute-done.7.last_ref = bf16[2,384,128]{2,1,0:T(8,128)(2,1)S(1)} collective-permute-done((bf16[2,384,128]{2,1,0:T(8,128)(2,1)S(1)}, bf16[2,384,128]{2,1,0:T(8,128)(2,1)S(1)}, u32[]{:S(2)}, u32[]{:S(2)}) %collective-permute-start.7) | collective-permute-done | bytes 196640 | tf_op jit(solution)/shard_map/ppermute | solution.py:38
  60.4 4.8 %all-to-all-start.1 = ((bf16[4,528,512]{2,1,0:T(8,128)(2,1)}), bf16[4,528,512]{2,1,0:T(8,128)(2,1)S(1)}, u32[]{:S(2)}, u32[]{:S(2)}) async-start(bf16[4,528,512]{2,1,0:T(8,128)(2,1)} %get-tuple-element.36), calls=%async_computation.1 | async-start | bytes 4325376 | tf_op jit(solution)/shard_map/all_to_all | solution.py:49
  66.9 5.3 %collective-permute-start = (bf16[2,256,128]{2,1,0:T(8,128)(2,1)S(1)}, bf16[2,256,128]{2,1,0:T(8,128)(2,1)S(1)}, u32[]{:S(2)}, u32[]{:S(2)}) collective-permute-start(bf16[2,256,128]{2,1,0:T(8,128)(2,1)S(1)} %get-tuple-element.28), channel_id=1, source_target_pairs={{0,4},{2,6},{4,0},{6,2},{1,5},{3,7},{5,1},{7,3},{8,12},{10,14},{12... | collective-permute-start | bytes 393224 | tf_op jit(solution)/shard_map/ppermute | solution.py:38
  72.2 5.4 %collective-permute-done = bf16[2,256,128]{2,1,0:T(8,128)(2,1)S(1)} collective-permute-done((bf16[2,256,128]{2,1,0:T(8,128)(2,1)S(1)}, bf16[2,256,128]{2,1,0:T(8,128)(2,1)S(1)}, u32[]{:S(2)}, u32[]{:S(2)}) %collective-permute-start) | collective-permute-done | bytes 131104 | tf_op jit(solution)/shard_map/ppermute | solution.py:38
  80.2 4.2 %collective-permute-done.1 = bf16[2,256,128]{2,1,0:T(8,128)(2,1)S(1)} collective-permute-done((bf16[2,256,128]{2,1,0:T(8,128)(2,1)S(1)}, bf16[2,256,128]{2,1,0:T(8,128)(2,1)S(1)}, u32[]{:S(2)}, u32[]{:S(2)}) %collective-permute-start.1) | collective-permute-done | bytes 131104 | tf_op jit(solution)/shard_map/ppermute | solution.py:38
  84.5 10.9 %collective-permute-start.2 = (bf16[4,256,128]{2,1,0:T(8,128)(2,1)S(1)}, bf16[4,256,128]{2,1,0:T(8,128)(2,1)}, u32[]{:S(2)}, u32[]{:S(2)}) collective-permute-start(bf16[4,256,128]{2,1,0:T(8,128)(2,1)S(1)} %pad_maximum_fusion.refs_0_), channel_id=1, source_target_pairs={{0,64},{64,128},{128,0},{1,65},{65,129},{129,1},{2,66},{66,130},{1... | collective-permute-start | bytes 786440 | tf_op jit(solution)/shard_map/ppermute | solution.py:33
  95.5 3.8 %collective-permute-start.3 = (bf16[4,256,128]{2,1,0:T(8,128)(2,1)S(1)}, bf16[4,256,128]{2,1,0:T(8,128)(2,1)}, u32[]{:S(2)}, u32[]{:S(2)}) collective-permute-start(bf16[4,256,128]{2,1,0:T(8,128)(2,1)S(1)} %pad_maximum_fusion.refs_0_), channel_id=1, source_target_pairs={{0,128},{64,0},{128,64},{1,129},{65,1},{129,65},{2,130},{66,2},{13... | collective-permute-start | bytes 786440 | tf_op jit(solution)/shard_map/ppermute | solution.py:33
  101.1 8.2 %all-to-all-start.2 = ((bf16[12,256,128]{2,1,0:T(8,128)(2,1)}), bf16[12,256,128]{2,1,0:T(8,128)(2,1)S(1)}, u32[]{:S(2)}, u32[]{:S(2)}) async-start(bf16[12,256,128]{2,1,0:T(8,128)(2,1)} %shard_map.177), calls=%async_computation.2 | async-start | bytes 1572864 | tf_op jit(solution)/shard_map/all_to_all | solution.py:49
  109.4 16.6 %collective-permute-done.3.refs_2_ = bf16[4,256,128]{2,1,0:T(8,128)(2,1)} collective-permute-done((bf16[4,256,128]{2,1,0:T(8,128)(2,1)S(1)}, bf16[4,256,128]{2,1,0:T(8,128)(2,1)}, u32[]{:S(2)}, u32[]{:S(2)}) %collective-permute-start.3) | collective-permute-done | bytes 262176 | tf_op jit(solution)/shard_map/ppermute | solution.py:33
  127.3 3.4 %collective-permute-start.4 = (bf16[4,560,128]{2,1,0:T(8,128)(2,1)S(1)}, bf16[4,560,128]{2,1,0:T(8,128)(2,1)S(1)}, u32[]{:S(2)}, u32[]{:S(2)}) collective-permute-start(bf16[4,560,128]{2,1,0:T(8,128)(2,1)S(1)} %shard_map.171.refs_0_), channel_id=1, source_target_pairs={{0,192},{192,384},{384,576},{576,0},{1,193},{193,385},{385,577},{5... | collective-permute-start | bytes 1720328 | tf_op jit(solution)/shard_map/ppermute | solution.py:33
  133.1 9.8 %collective-permute-done.4.refs_1_ = bf16[4,560,128]{2,1,0:T(8,128)(2,1)S(1)} collective-permute-done((bf16[4,560,128]{2,1,0:T(8,128)(2,1)S(1)}, bf16[4,560,128]{2,1,0:T(8,128)(2,1)S(1)}, u32[]{:S(2)}, u32[]{:S(2)}) %collective-permute-start.4) | collective-permute-done | bytes 573472 | tf_op jit(solution)/shard_map/ppermute | solution.py:33
  142.9 3.4 %collective-permute-start.5 = (bf16[4,560,128]{2,1,0:T(8,128)(2,1)S(1)}, bf16[4,560,128]{2,1,0:T(8,128)(2,1)S(1)}, u32[]{:S(2)}, u32[]{:S(2)}) collective-permute-start(bf16[4,560,128]{2,1,0:T(8,128)(2,1)S(1)} %collective-permute-done.4.refs_1_), channel_id=1, source_target_pairs={{0,192},{192,384},{384,576},{576,0},{1,193},{193,385},{385,577},{5... | collective-permute-start | bytes 1720328 | tf_op jit(solution)/shard_map/ppermute | solution.py:33
  149.0 8.8 %collective-permute-done.5.weight_ref = bf16[4,560,128]{2,1,0:T(8,128)(2,1)S(1)} collective-permute-done((bf16[4,560,128]{2,1,0:T(8,128)(2,1)S(1)}, bf16[4,560,128]{2,1,0:T(8,128)(2,1)S(1)}, u32[]{:S(2)}, u32[]{:S(2)}) %collective-permute-start.5) | collective-permute-done | bytes 573472 | tf_op jit(solution)/shard_map/ppermute | solution.py:33
  160.1 3.2 %collective-permute-start.10 = (bf16[2,384,128]{2,1,0:T(8,128)(2,1)S(1)}, bf16[2,384,128]{2,1,0:T(8,128)(2,1)S(1)}, u32[]{:S(2)}, u32[]{:S(2)}) collective-permute-start(bf16[2,384,128]{2,1,0:T(8,128)(2,1)S(1)} %get-tuple-element.34), channel_id=1, source_target_pairs={{0,4},{2,6},{4,0},{6,2},{1,5},{3,7},{5,1},{7,3},{8,12},{10,14},{12... | collective-permute-start | bytes 589832 | tf_op jit(solution)/shard_map/ppermute | solution.py:38
  164.2 6.6 %collective-permute-done.10 = bf16[2,384,128]{2,1,0:T(8,128)(2,1)S(1)} collective-permute-done((bf16[2,384,128]{2,1,0:T(8,128)(2,1)S(1)}, bf16[2,384,128]{2,1,0:T(8,128)(2,1)S(1)}, u32[]{:S(2)}, u32[]{:S(2)}) %collective-permute-start.10) | collective-permute-done | bytes 196640 | tf_op jit(solution)/shard_map/ppermute | solution.py:38
  173.7 3.6 %collective-permute-done.11 = bf16[384,128]{1,0:T(8,128)(2,1)S(1)} collective-permute-done((bf16[384,128]{1,0:T(8,128)(2,1)S(1)}, bf16[384,128]{1,0:T(8,128)(2,1)S(1)}, u32[]{:S(2)}, u32[]{:S(2)}) %collective-permute-start.11) | collective-permute-done | bytes 98336 | tf_op jit(solution)/shard_map/ppermute | solution.py:38
  180.5 13.9 %all-to-all-start.4 = ((f32[12,2,128]{2,1,0:T(2,128)}), f32[12,2,128]{2,1,0:T(2,128)S(1)}, u32[]{:S(2)}, u32[]{:S(2)}) async-start(f32[12,2,128]{2,1,0:T(2,128)} %get-tuple-element.40), calls=%async_computation.4 | async-start | bytes 24576 | tf_op jit(solution)/shard_map/all_to_all | solution.py:49
  196.2 6.8 %all-to-all-done.4 = f32[12,2,128]{2,1,0:T(2,128)S(1)} async-done(((f32[12,2,128]{2,1,0:T(2,128)}), f32[12,2,128]{2,1,0:T(2,128)S(1)}, u32[]{:S(2)}, u32[]{:S(2)}) %all-to-all-start.4) | async-done | bytes 12320 | tf_op jit(solution)/shard_map/all_to_all | solution.py:49
  203.8 5.6 %all-to-all-start.3 = ((bf16[32,2,688]{2,1,0:T(2,128)(2,1)}), bf16[32,2,688]{2,1,0:T(2,128)(2,1)S(1)}, u32[]{:S(2)}, u32[]{:S(2)}) async-start(bf16[32,2,688]{2,1,0:T(2,128)(2,1)} %broadcast_in_dim.7), calls=%async_computation.3 | async-start | bytes 196608 | tf_op jit(solution)/shard_map/all_to_all | solution.py:49
  211.5 8.7 %all-to-all-done.3 = bf16[32,2,688]{2,1,0:T(2,128)(2,1)S(1)} async-done(((bf16[32,2,688]{2,1,0:T(2,128)(2,1)}), bf16[32,2,688]{2,1,0:T(2,128)(2,1)S(1)}, u32[]{:S(2)}, u32[]{:S(2)}) %all-to-all-start.3) | async-done | bytes 88096 | tf_op jit(solution)/shard_map/all_to_all | solution.py:49
  (80 shorter events, 41.9 us)
Async XLA Ops:
  2.6 30.2 %all-to-all-start = ((bf16[8,128,384]{2,1,0:T(8,128)(2,1)}), bf16[8,128,384]{2,1,0:T(8,128)(2,1)S(1)}, u32[]{:S(2)}, u32[]{:S(2)}) async-start(bf16[8,128,384]{2,1,0:T(8,128)(2,1)} %shard_map.172), calls=%async_computation | async-start | bytes 1572864 | tf_op jit(solution)/shard_map/all_to_all | solution.py:49
  32.8 25.5 %collective-permute-start.8 = (bf16[8,128,384]{2,1,0:T(8,128)(2,1)S(1)}, bf16[8,128,384]{2,1,0:T(8,128)(2,1)S(1)}, u32[]{:S(2)}, u32[]{:S(2)}) collective-permute-start(bf16[8,128,384]{2,1,0:T(8,128)(2,1)S(1)} %all-to-all-done.part_ref), channel_id=1, source_target_pairs={{0,1},{1,0},{2,3},{3,2},{4,5},{5,4},{6,7},{7,6},{8,9},{9,8},{10,11... | collective-permute-start | bytes 2359304 | tf_op jit(solution)/shard_map/ppermute | solution.py:33
  36.8 11.6 %collective-permute-start.6 = (bf16[384,128]{1,0:T(8,128)(2,1)S(1)}, bf16[384,128]{1,0:T(8,128)(2,1)S(1)}, u32[]{:S(2)}, u32[]{:S(2)}) collective-permute-start(bf16[384,128]{1,0:T(8,128)(2,1)S(1)} %convolution_convert_fusion.att_ref), channel_id=1, source_target_pairs={{0,4},{2,6},{4,0},{6,2},{1,5},{3,7},{5,1},{7,3},{8,12},{10,14},{12... | collective-permute-start | bytes 294920 | tf_op jit(solution)/shard_map/ppermute | solution.py:38
  48.5 7.8 %collective-permute-start.7 = (bf16[2,384,128]{2,1,0:T(8,128)(2,1)S(1)}, bf16[2,384,128]{2,1,0:T(8,128)(2,1)S(1)}, u32[]{:S(2)}, u32[]{:S(2)}) collective-permute-start(bf16[2,384,128]{2,1,0:T(8,128)(2,1)S(1)} %pad_maximum_fusion.1), channel_id=1, source_target_pairs={{0,2},{2,0},{4,6},{6,4},{1,3},{3,1},{5,7},{7,5},{8,10},{10,8},{12,... | collective-permute-start | bytes 589832 | tf_op jit(solution)/shard_map/ppermute | solution.py:38
  60.4 38.8 %all-to-all-start.1 = ((bf16[4,528,512]{2,1,0:T(8,128)(2,1)}), bf16[4,528,512]{2,1,0:T(8,128)(2,1)S(1)}, u32[]{:S(2)}, u32[]{:S(2)}) async-start(bf16[4,528,512]{2,1,0:T(8,128)(2,1)} %get-tuple-element.36), calls=%async_computation.1 | async-start | bytes 4325376 | tf_op jit(solution)/shard_map/all_to_all | solution.py:49
  66.9 10.7 %collective-permute-start = (bf16[2,256,128]{2,1,0:T(8,128)(2,1)S(1)}, bf16[2,256,128]{2,1,0:T(8,128)(2,1)S(1)}, u32[]{:S(2)}, u32[]{:S(2)}) collective-permute-start(bf16[2,256,128]{2,1,0:T(8,128)(2,1)S(1)} %get-tuple-element.28), channel_id=1, source_target_pairs={{0,4},{2,6},{4,0},{6,2},{1,5},{3,7},{5,1},{7,3},{8,12},{10,14},{12... | collective-permute-start | bytes 393224 | tf_op jit(solution)/shard_map/ppermute | solution.py:38
  77.6 6.9 %collective-permute-start.1 = (bf16[2,256,128]{2,1,0:T(8,128)(2,1)S(1)}, bf16[2,256,128]{2,1,0:T(8,128)(2,1)S(1)}, u32[]{:S(2)}, u32[]{:S(2)}) collective-permute-start(bf16[2,256,128]{2,1,0:T(8,128)(2,1)S(1)} %pad_maximum_fusion.2), channel_id=1, source_target_pairs={{0,2},{2,0},{4,6},{6,4},{1,3},{3,1},{5,7},{7,5},{8,10},{10,8},{12,... | collective-permute-start | bytes 393224 | tf_op jit(solution)/shard_map/ppermute | solution.py:38
  84.5 24.8 %collective-permute-start.2 = (bf16[4,256,128]{2,1,0:T(8,128)(2,1)S(1)}, bf16[4,256,128]{2,1,0:T(8,128)(2,1)}, u32[]{:S(2)}, u32[]{:S(2)}) collective-permute-start(bf16[4,256,128]{2,1,0:T(8,128)(2,1)S(1)} %pad_maximum_fusion.refs_0_), channel_id=1, source_target_pairs={{0,64},{64,128},{128,0},{1,65},{65,129},{129,1},{2,66},{66,130},{1... | collective-permute-start | bytes 786440 | tf_op jit(solution)/shard_map/ppermute | solution.py:33
  95.5 30.5 %collective-permute-start.3 = (bf16[4,256,128]{2,1,0:T(8,128)(2,1)S(1)}, bf16[4,256,128]{2,1,0:T(8,128)(2,1)}, u32[]{:S(2)}, u32[]{:S(2)}) collective-permute-start(bf16[4,256,128]{2,1,0:T(8,128)(2,1)S(1)} %pad_maximum_fusion.refs_0_), channel_id=1, source_target_pairs={{0,128},{64,0},{128,64},{1,129},{65,1},{129,65},{2,130},{66,2},{13... | collective-permute-start | bytes 786440 | tf_op jit(solution)/shard_map/ppermute | solution.py:33
  101.1 45.2 %copy-start.1 = (bf16[8,128,384]{2,1,0:T(8,128)(2,1)S(1)}, bf16[8,128,384]{2,1,0:T(8,128)(2,1)}, u32[]{:S(2)}) copy-start(bf16[8,128,384]{2,1,0:T(8,128)(2,1)} %get-tuple-element.30.near_ref) | copy-start | bytes 2359300
  101.1 45.2 %copy-start.2 = (bf16[8,128,384]{2,1,0:T(8,128)(2,1)S(1)}, bf16[8,128,384]{2,1,0:T(8,128)(2,1)}, u32[]{:S(2)}) copy-start(bf16[8,128,384]{2,1,0:T(8,128)(2,1)} %get-tuple-element.32.far_ref) | copy-start | bytes 2359300
  101.1 76.4 %all-to-all-start.2 = ((bf16[12,256,128]{2,1,0:T(8,128)(2,1)}), bf16[12,256,128]{2,1,0:T(8,128)(2,1)S(1)}, u32[]{:S(2)}, u32[]{:S(2)}) async-start(bf16[12,256,128]{2,1,0:T(8,128)(2,1)} %shard_map.177), calls=%async_computation.2 | async-start | bytes 1572864 | tf_op jit(solution)/shard_map/all_to_all | solution.py:49
  127.3 15.6 %collective-permute-start.4 = (bf16[4,560,128]{2,1,0:T(8,128)(2,1)S(1)}, bf16[4,560,128]{2,1,0:T(8,128)(2,1)S(1)}, u32[]{:S(2)}, u32[]{:S(2)}) collective-permute-start(bf16[4,560,128]{2,1,0:T(8,128)(2,1)S(1)} %shard_map.171.refs_0_), channel_id=1, source_target_pairs={{0,192},{192,384},{384,576},{576,0},{1,193},{193,385},{385,577},{5... | collective-permute-start | bytes 1720328 | tf_op jit(solution)/shard_map/ppermute | solution.py:33
  130.7 15.6 %collective-permute-start.9 = (bf16[4,560,128]{2,1,0:T(8,128)(2,1)S(1)}, bf16[4,560,128]{2,1,0:T(8,128)(2,1)S(1)}, u32[]{:S(2)}, u32[]{:S(2)}) collective-permute-start(bf16[4,560,128]{2,1,0:T(8,128)(2,1)S(1)} %shard_map.171.refs_0_), channel_id=1, source_target_pairs={{0,576},{192,0},{384,192},{576,384},{1,577},{193,1},{385,193},{577... | collective-permute-start | bytes 1720328 | tf_op jit(solution)/shard_map/ppermute | solution.py:33
  142.9 14.8 %collective-permute-start.5 = (bf16[4,560,128]{2,1,0:T(8,128)(2,1)S(1)}, bf16[4,560,128]{2,1,0:T(8,128)(2,1)S(1)}, u32[]{:S(2)}, u32[]{:S(2)}) collective-permute-start(bf16[4,560,128]{2,1,0:T(8,128)(2,1)S(1)} %collective-permute-done.4.refs_1_), channel_id=1, source_target_pairs={{0,192},{192,384},{384,576},{576,0},{1,193},{193,385},{385,577},{5... | collective-permute-start | bytes 1720328 | tf_op jit(solution)/shard_map/ppermute | solution.py:33
  148.9 14.4 %copy-start.15 = (f32[128]{0:T(128)S(1)}, f32[128]{0:T(128)}, u32[]{:S(2)}) copy-start(f32[128]{0:T(128)} %param.21) | copy-start | bytes 1540
  148.9 23.9 %copy-start.8 = (bf16[688,128]{1,0:T(8,128)(2,1)S(1)}, bf16[688,128]{1,0:T(8,128)(2,1)}, u32[]{:S(2)}) copy-start(bf16[688,128]{1,0:T(8,128)(2,1)} %param.16) | copy-start | bytes 528388
  148.9 23.9 %copy-start.12 = (f32[688]{0:T(1024)S(1)}, f32[688]{0:T(1024)}, u32[]{:S(2)}) copy-start(f32[688]{0:T(1024)} %param.17) | copy-start | bytes 8260
  148.9 23.9 %copy-start.16 = (f32[128]{0:T(128)S(1)}, f32[128]{0:T(128)}, u32[]{:S(2)}) copy-start(f32[128]{0:T(128)} %param.18) | copy-start | bytes 1540
  160.1 49.3 %copy-start.6 = (f32[384,384]{0,1:T(8,128)S(1)}, f32[384,384]{0,1:T(8,128)}, u32[]{:S(2)}) copy-start(f32[384,384]{0,1:T(8,128)} %copy-done.5) | copy-start | bytes 1769476
  160.1 10.7 %collective-permute-start.10 = (bf16[2,384,128]{2,1,0:T(8,128)(2,1)S(1)}, bf16[2,384,128]{2,1,0:T(8,128)(2,1)S(1)}, u32[]{:S(2)}, u32[]{:S(2)}) collective-permute-start(bf16[2,384,128]{2,1,0:T(8,128)(2,1)S(1)} %get-tuple-element.34), channel_id=1, source_target_pairs={{0,4},{2,6},{4,0},{6,2},{1,5},{3,7},{5,1},{7,3},{8,12},{10,14},{12... | collective-permute-start | bytes 589832 | tf_op jit(solution)/shard_map/ppermute | solution.py:38
  170.9 6.5 %collective-permute-start.11 = (bf16[384,128]{1,0:T(8,128)(2,1)S(1)}, bf16[384,128]{1,0:T(8,128)(2,1)S(1)}, u32[]{:S(2)}, u32[]{:S(2)}) collective-permute-start(bf16[384,128]{1,0:T(8,128)(2,1)S(1)} %fusion.11), channel_id=1, source_target_pairs={{0,2},{2,0},{4,6},{6,4},{1,3},{3,1},{5,7},{7,5},{8,10},{10,8},{12,... | collective-permute-start | bytes 294920 | tf_op jit(solution)/shard_map/ppermute | solution.py:38
  180.5 22.6 %all-to-all-start.4 = ((f32[12,2,128]{2,1,0:T(2,128)}), f32[12,2,128]{2,1,0:T(2,128)S(1)}, u32[]{:S(2)}, u32[]{:S(2)}) async-start(f32[12,2,128]{2,1,0:T(2,128)} %get-tuple-element.40), calls=%async_computation.4 | async-start | bytes 24576 | tf_op jit(solution)/shard_map/all_to_all | solution.py:49
  203.8 16.4 %all-to-all-start.3 = ((bf16[32,2,688]{2,1,0:T(2,128)(2,1)}), bf16[32,2,688]{2,1,0:T(2,128)(2,1)S(1)}, u32[]{:S(2)}, u32[]{:S(2)}) async-start(bf16[32,2,688]{2,1,0:T(2,128)(2,1)} %broadcast_in_dim.7), calls=%async_computation.3 | async-start | bytes 196608 | tf_op jit(solution)/shard_map/all_to_all | solution.py:49
  (11 other events, 74.8 us)
